TPU v7x, 32 devices: a whole 2x2x4 slice. The times are simulated.
32 devices in a mesh: seg: 16 (over z, y, x), slab: 2 (over core).
Axes of the slice: x: 2, y: 2, z: 4, core: 2. Of those that a mesh axis runs over, the one named last changes fastest.
Arguments:
- block: float32 [16, 4, 16, 4096], P('seg', None, 'slab'), may hold values from -6 to 6
- base_velocity: bfloat16 [16, 8, 2, 16, 4096], P('seg', None, None, 'slab'), may hold values from -6 to 6
Outputs:
- new_block: float32 [16, 4, 16, 4096], P('seg', None, 'slab')
All inputs are finite; a program needn't handle non-finite values.
Results may differ from a plain program's by a relative error of at most 0.0003.
Values may be sent and summed in bfloat16 or wider, within the bound.
No kernel may reach another device: no remote copies, remote signals or barrier semaphores. Data moves between devices by JAX's collectives and lax.ppermute only.
A program may use at most 64 MiB of HBM per device.

v0:
```python
import functools

import jax
import jax.numpy as jnp
from jax import lax
from jax.experimental import pallas as pl
from jax.experimental.pallas import tpu as pltpu
from jax.sharding import PartitionSpec as P


HOPS = 4
SUB = 8
LANE = 128
VMEM = pl.BlockSpec(memory_space=pltpu.VMEM)


def tiled(rows):
    lead, (height, width) = rows.shape[:-2], rows.shape[-2:]
    cut = rows.reshape(lead + (height, width // LANE, LANE))
    return jnp.swapaxes(cut, -3, -2)


def untiled(tiles):
    lead, (count, height, lane) = tiles.shape[:-3], tiles.shape[-3:]
    return jnp.swapaxes(tiles, -3, -2).reshape(lead + (height, count * lane))


def advance(velocity, ping, pong, pieces):
    depth, _, columns, height, _ = velocity[0].shape
    rows = pieces * height
    lane = lax.broadcasted_iota(jnp.int32, (SUB, LANE), 1)
    first, last = lane == 0, lane == LANE - 1

    def step(k, source, target):
        for b in range(rows // SUB):
            piece, at = divmod(SUB * b, height)
            rows_at = pl.ds(SUB + SUB * b, SUB)
            here = [source[j % columns, rows_at, :] for j in (-1, 0, 1)]
            for j in range(columns):
                left, centre, right = here
                west = pltpu.roll(jnp.where(last, left, centre), 1, 1)
                east = pltpu.roll(jnp.where(first, right, centre), LANE - 1, 1)
                up = source[j, pl.ds(SUB + 1 + SUB * b, SUB), :]
                down = source[j, pl.ds(SUB - 1 + SUB * b, SUB), :]
                speed_x = velocity[piece][k, 0, j, pl.ds(at, SUB), :].astype(jnp.float32)
                speed_y = velocity[piece][k, 1, j, pl.ds(at, SUB), :].astype(jnp.float32)
                carried = speed_x * (west - east) + speed_y * (down - up)
                place(target, rows, j, b, 0.9 * centre + ((west + east) + (up + down)) + 0.25 * carried)
                here = [centre, right, source[(j + 2) % columns, rows_at, :]]

    def pair(i, carry):
        step(2 * i, ping, pong)
        step(2 * i + 1, pong, ping)
        return carry

    lax.fori_loop(0, depth // 2, pair, 0)
    if depth % 2:
        step(depth - 1, ping, pong)
        return pong
    return ping


def place(ref, rows, j, b, value):
    ref[j, pl.ds(SUB + SUB * b, SUB), :] = value
    if b == 0:
        ref[j, pl.ds(SUB + rows, 1), :] = value[:1]
    if b == rows // SUB - 1:
        ref[j, pl.ds(SUB - 1, 1), :] = value[SUB - 1 :]


def tiles_of(pieces, columns, height):
    for j in range(columns):
        for b in range(pieces * height // SUB):
            piece, at = divmod(SUB * b, height)
            yield piece, j, pl.ds(at, SUB), b, (piece * columns + j) * (height // SUB) + at // SUB


TOP = 13.0


def take_in(cases, use):
    def run(message, previous):
        count = message.shape[0] - 1
        back = jnp.exp2(message[count] - TOP)
        pieces, columns, height, _ = previous.shape
        for piece, j, at, b, m in tiles_of(pieces, columns, height):
            use(piece, j, at, b, message[m] * back - previous[piece, j, at, :])

    for chosen, message, previous in cases:
        pl.when(chosen)(functools.partial(run, message, previous))


def ends_of_ring():
    here = lax.axis_index("seg")
    return here == lax.axis_size("seg") - 1, here == 0


def propagate_kernel(pieces, index, first, last, final, *refs):
    refs = list(refs)
    take = lambda count: [refs.pop(0) for _ in range(count)]
    velocity = take(pieces)
    depth, _, columns, height, _ = velocity[0].shape
    rows, count = pieces * height, pieces * columns * height // SUB
    if first:
        previous = take(pieces)
    else:
        previous, missed, message = take(3)
        wrapped = None if last else take(1)[0]
        (start,) = take(1)
    (sent,) = take(1)
    error = None if final else take(1)[0]
    ping, pong = refs
    at_last, at_first = ends_of_ring()

    @pl.when(at_last if last else jnp.logical_not(at_last))
    def _():
        def use(piece, j, at, b, value):
            start[piece, j, at, :] = value
            place(ping, rows, j, b, value)

        if first:
            for piece, j, at, b, m in tiles_of(pieces, columns, height):
                place(ping, rows, j, b, previous[piece][index, j, at, :])
        elif last:
            take_in([(at_last, message, previous)], use)
        else:
            take_in([(at_first, wrapped, previous), (jnp.logical_not(at_first), message, previous)], use)

        done = advance(velocity, ping, pong, pieces)
        largest = None
        for piece, j, at, b, m in tiles_of(pieces, columns, height):
            value = 0.2**depth * done[j, pl.ds(SUB + SUB * b, SUB), :]
            if not first:
                value = value + missed[m]
            sent[m] = value
            size = jnp.abs(value)
            largest = size if largest is None else jnp.maximum(largest, size)
        largest = jnp.broadcast_to(jnp.max(largest, axis=(0, 1), keepdims=True), (SUB, LANE))
        power = jnp.clip(jnp.floor(jnp.log2(largest)), -100.0, 100.0)
        scale, back = jnp.exp2(TOP - power), jnp.exp2(power - TOP)
        sent[count] = power
        for m in range(count):
            value = sent[m]
            scaled = value * scale
            wide = scaled * 8193.0
            short = wide - (wide - scaled)
            sent[m] = short
            if not final:
                error[m] = short * back - value


@functools.partial(jax.jit, static_argnames=("index", "last", "final"))
def propagate(velocity, state, index=0, last=False, final=False):
    pieces = len(velocity)
    _, _, columns, height, lane = velocity[0].shape
    count = pieces * columns * height // SUB
    first = isinstance(state, list)
    shape = lambda *s: jax.ShapeDtypeStruct(s + (lane,), jnp.float32)
    outs = ([] if first else [shape(pieces, columns, height)]) + [shape(count + 1, SUB)]
    outs = outs + ([] if final else [shape(count, SUB)])
    scratch = pltpu.VMEM((columns, pieces * height + 2 * SUB, lane), jnp.float32)
    args = [*velocity, *state]
    return pl.pallas_call(
        functools.partial(propagate_kernel, pieces, index, first, last, final),
        out_shape=outs,
        in_specs=[VMEM] * len(args),
        out_specs=[VMEM] * len(outs),
        scratch_shapes=[scratch, scratch],
        compiler_params=pltpu.CompilerParams(vmem_limit_bytes=16 << 20),
        name="propagate_last" if last else "propagate",
    )(*args)


def residual_kernel(message, wrapped, previous, previous_last, *outs):
    def use(piece, j, at, b, value):
        outs[piece][0, j, at, :] = value

    at_last, at_first = ends_of_ring()
    rest = jnp.logical_not(jnp.logical_or(at_last, at_first))
    cases = [(at_last, message, previous_last), (at_first, wrapped, previous), (rest, message, previous)]
    take_in(cases, use)


@jax.jit
def last_residual(*state):
    pieces, columns, height, lane = state[2].shape
    return pl.pallas_call(
        residual_kernel,
        out_shape=[jax.ShapeDtypeStruct((1, columns, height, lane), jnp.float32)] * pieces,
        in_specs=[VMEM] * len(state),
        out_specs=[VMEM] * pieces,
        compiler_params=pltpu.CompilerParams(vmem_limit_bytes=16 << 20),
        name="residual",
    )(*state)


def rows_kernel(pieces, index, *refs):
    velocity, previous, (moved, ping, pong) = refs[:pieces], refs[pieces : 2 * pieces], refs[2 * pieces :]
    depth, _, columns, height, _ = velocity[0].shape
    for piece, j, at, b, _ in tiles_of(pieces, columns, height):
        place(ping, pieces * height, j, b, previous[piece][index, j, at, :])
    done = advance(velocity, ping, pong, pieces)
    for piece, j, at, b, _ in tiles_of(1, columns, height):
        moved[0, j, at, :] = 0.2**depth * done[j, pl.ds(SUB + SUB * b, SUB), :]


@functools.partial(jax.jit, static_argnames=("index",))
def propagate_rows(velocity, state, index):
    pieces = len(velocity)
    _, _, columns, height, lane = velocity[0].shape
    scratch = pltpu.VMEM((columns, pieces * height + 2 * SUB, lane), jnp.float32)
    return pl.pallas_call(
        functools.partial(rows_kernel, pieces, index),
        out_shape=jax.ShapeDtypeStruct((1, columns, height, lane), jnp.float32),
        in_specs=[VMEM] * (2 * pieces),
        out_specs=VMEM,
        scratch_shapes=[scratch, scratch],
        compiler_params=pltpu.CompilerParams(vmem_limit_bytes=16 << 20),
        name="propagate_rows",
    )(*velocity, *state)


def gram_kernel(share, *refs):
    residual, (gram, lines) = refs[:-2], refs[-2:]
    count = len(residual)
    _, columns, height, _ = residual[0].shape
    base = lax.axis_index("slab") * share
    sums = {}
    for j in range(columns):
        for at in range(0, height, SUB):
            values = [r[0, j, pl.ds(at, SUB), :] for r in residual]
            for p in range(count):
                for q in range(p + 1):
                    term = values[p] * values[q]
                    sums[p, q] = term if (p, q) not in sums else sums[p, q] + term
    for (p, q), total in sums.items():
        line = jnp.sum(total, axis=0, keepdims=True)
        a, b = lax.rem(base + p, count), lax.rem(base + q, count)
        lines[pl.ds(a * count + b, 1), :] = line
        if p != q:
            lines[pl.ds(b * count + a, 1), :] = line
    totals = jnp.where(diagonal(count), jnp.sum(lines[...], axis=1, keepdims=True), 0.0)
    gram[...] = jnp.broadcast_to(jnp.sum(totals, axis=0, keepdims=True), gram.shape)


def diagonal(count):
    shape = (count * count, LANE)
    return lax.broadcasted_iota(jnp.int32, shape, 0) == lax.broadcasted_iota(jnp.int32, shape, 1)


def local_gram(share, residual, copies):
    count = len(residual)
    return pl.pallas_call(
        functools.partial(gram_kernel, share),
        out_shape=jax.ShapeDtypeStruct((copies, LANE), jnp.float32),
        in_specs=[VMEM] * count,
        out_specs=VMEM,
        scratch_shapes=[pltpu.VMEM((count * count, LANE), jnp.float32)],
        compiler_params=pltpu.CompilerParams(vmem_limit_bytes=16 << 20),
        name="gram",
    )(*residual)


def solve_kernel(share, gram, *refs):
    residual, out = refs[:-1], refs[-1]
    count, columns, height, lane = out.shape
    line = jnp.broadcast_to(jnp.sum(gram[...], axis=0, keepdims=True), (count * count, lane))
    total = jnp.sum(jnp.where(diagonal(count), line, 0.0), axis=1, keepdims=True)
    entry = lambda a, b: total[a * count + b : a * count + b + 1, :]
    lower, inverse = {}, {}
    for a in range(count):
        for b in range(a + 1):
            value = entry(a, b)
            for k in range(b):
                value = value - lower[a, k] * lower[b, k]
            lower[a, b] = jnp.sqrt(value) if a == b else value / lower[b, b]
    for a in range(count):
        inverse[a, a] = 1.0 / lower[a, a]
        for b in range(a):
            value = lower[a, b] * inverse[b, b]
            for k in range(b + 1, a):
                value = value + lower[a, k] * inverse[k, b]
            inverse[a, b] = -value / lower[a, a]
    factors = {at: jnp.broadcast_to(value, (SUB, lane)) for at, value in inverse.items()}

    def finish(place):
        for j in range(columns):
            for at in range(0, height, SUB):
                values = [residual[place[a]][0, j, pl.ds(at, SUB), :] for a in range(count)]
                for a in range(count):
                    value = factors[a, 0] * values[0]
                    for b in range(1, a + 1):
                        value = value + factors[a, b] * values[b]
                    out[a, j, pl.ds(at, SUB), :] = value

    base = lax.axis_index("slab") * share
    for turn in range(0, count, share or count):
        pl.when(base == turn)(functools.partial(finish, [(a - turn) % count for a in range(count)]))


def solved(share, gram, residual):
    count, (_, columns, height, lane) = len(residual), residual[0].shape
    return pl.pallas_call(
        functools.partial(solve_kernel, share),
        out_shape=jax.ShapeDtypeStruct((count, columns, height, lane), jnp.float32),
        in_specs=[VMEM] * (1 + count),
        out_specs=VMEM,
        compiler_params=pltpu.CompilerParams(vmem_limit_bytes=16 << 20),
        name="solve",
    )(gram, *residual)


def from_slab(value, distance):
    size = lax.axis_size("slab")
    return lax.ppermute(value, "slab", [((i + distance) % size, i) for i in range(size)])


def to_next(value, segments=None):
    size = lax.axis_size("seg")
    return lax.ppermute(value, "seg", [(i, (i + 1) % size) for i in segments or range(size)])


def sent_short(message, segments=None):
    return to_next(message.astype(jnp.float16), segments).astype(jnp.float32)


def split_vectors(vectors, velocity):
    slabs, mine = lax.axis_size("slab"), lax.axis_index("slab")
    share = vectors.shape[0] // slabs

    def part(distance):
        at = lax.rem(mine + distance, slabs) * share
        return lax.dynamic_slice_in_dim(vectors, at, share, 0)

    start, speeds = [part(0)], [velocity]
    for d in range(1, slabs):
        start.append(from_slab(part(slabs - d), d))
        speeds.append(from_slab(velocity, d))
    end = lax.axis_size("seg") - 1
    previous = [jnp.concatenate([part[i : i + 1] for part in start], 0) for i in range(share)]
    own, ends = list(previous), list(previous)
    arrived, wrapped, missed, missed_end = [[None] * share for _ in range(4)]
    for hop in range(HOPS):
        for i in range(share):
            if hop == 0:
                state_end, state = start, start
            else:
                state_end = (ends[i], missed_end[i], arrived[i])
                state = (own[i], missed[i], arrived[i], wrapped[i])
            final, index = hop + 1 == HOPS, i if hop == 0 else 0
            out_end = list(propagate(speeds, state_end, index, last=True, final=final))
            out = list(propagate(speeds, state, index, final=final))
            if hop:
                ends[i], own[i] = out_end.pop(0), out.pop(0)
            if not final:
                missed_end[i], missed[i] = out_end.pop(), out.pop()
            sent_end, sent = out_end[0], out[0]
            wrapped[i] = sent_short(sent_end, [end])
            arrived[i] = sent_short(sent, range(end))
    parts = [last_residual(arrived[i], wrapped[i], own[i], ends[i]) for i in range(share)]
    residual = []
    for d in range(slabs):
        for i in range(share):
            part_i = parts[i][(slabs - d) % slabs]
            residual.append(from_slab(part_i, d) if d else part_i)
    return share, residual


def split_rows(vectors, velocity):
    depth, height = velocity.shape[0], vectors.shape[2]

    def pieces(value):
        after = value[..., :depth, :]
        before = value[..., height - depth :, :]
        return [value, from_slab(after, 1), from_slab(before, -1)]

    speeds = pieces(velocity)
    begun = vectors
    for _ in range(HOPS):
        state = pieces(begun)
        arrived = [to_next(propagate_rows(speeds, state, i)) for i in range(vectors.shape[0])]
        begun = jnp.concatenate(arrived, 0) - begun
    return 0, [begun[i : i + 1] for i in range(vectors.shape[0])]


def shards(block, base_velocity):
    vectors, velocity = tiled(block[0]), tiled(base_velocity[0])
    even = vectors.shape[0] % lax.axis_size("slab") == 0
    share, residual = (split_vectors if even else split_rows)(vectors, velocity)
    axes = ("seg", "slab")
    gram = local_gram(share, residual, lax.axis_size("seg") * lax.axis_size("slab"))
    gram = lax.all_to_all(gram, axes, 0, 0, tiled=True)
    return untiled(solved(share, gram, residual))[None]


def solution(mesh):
    placed = (P("seg", None, "slab", None), P("seg", None, None, "slab", None))
    return jax.shard_map(
        shards, mesh=mesh, in_specs=placed, out_specs=P("seg", None, "slab", None), check_vma=False
    )
```

profile of v0, /device:TPU:0, one launch (start us, length us, event | category | flops | bytes accessed | tf_op | source)
XLA Modules:
  0.0 76.5 jit_solution(13669561609588224484)
XLA Ops:
  1.8 1.6 %collective-permute-done.1.refs_3_ = f32[2,32,8,128]{3,2,1,0:T(8,128)S(1)} collective-permute-done((f32[2,32,8,128]{3,2,1,0:T(8,128)S(1)}, f32[2,32,8,128]{3,2,1,0:T(8,128)S(1)}, u32[]{:S(2)}, u32[]{:S(2)}) %collective-permute-start.1) | collective-permute-done | bytes 262176 | tf_op jit(solution)/shard_map/ppermute | solution.py:315
  4.7 1.6 %propagate.12 = (f32[65,8,128]{2,1,0:T(8,128)S(1)}, f32[64,8,128]{2,1,0:T(8,128)S(1)}) custom-call(bf16[8,2,32,8,128]{4,3,2,1,0:T(8,128)(2,1)S(1)} %bitcast.17, bf16[8,2,32,8,128]{4,3,2,1,0:T(8,128)(2,1)S(1)} %collective-permute-done.refs_1_, f32[2,32,8,128]{3,2,1,0:T(8,128)S(1)} %get-tuple-element.93.refs_2_, ...), custom_call_target="tpu_custom_call" | custom-call | tf_op jit(solution)/shard_map/jit(propagate)/propagate/pallas_call | solution.py:163
  6.4 4.1 %collective-permute-start.10 = (f16[65,8,128]{2,1,0:T(8,128)(2,1)S(1)}, f16[65,8,128]{2,1,0:T(8,128)(2,1)S(1)}, u32[]{:S(2)}, u32[]{:S(2)}) collective-permute-start(f16[65,8,128]{2,1,0:T(8,128)(2,1)S(1)} %convert_element_type.112), channel_id=1, source_target_pairs={{0,2},{2,4},{4,6},{6,8},{8,10},{10,12},{12,14},{14,16},{16,18},{18... | collective-permute-start | bytes 399368 | tf_op jit(solution)/shard_map/ppermute | solution.py:320
  10.6 1.6 %propagate.8 = (f32[65,8,128]{2,1,0:T(8,128)S(1)}, f32[64,8,128]{2,1,0:T(8,128)S(1)}) custom-call(bf16[8,2,32,8,128]{4,3,2,1,0:T(8,128)(2,1)S(1)} %bitcast.19, bf16[8,2,32,8,128]{4,3,2,1,0:T(8,128)(2,1)S(1)} %collective-permute-done.refs_1_, f32[2,32,8,128]{3,2,1,0:T(8,128)S(1)} %get-tuple-element.93.refs_2_, ...), custom_call_target="tpu_custom_call" | custom-call | tf_op jit(solution)/shard_map/jit(propagate)/propagate/pallas_call | solution.py:163
  12.3 3.4 %collective-permute-start.2 = (f16[65,8,128]{2,1,0:T(8,128)(2,1)S(1)}, f16[65,8,128]{2,1,0:T(8,128)(2,1)S(1)}, u32[]{:S(2)}, u32[]{:S(2)}) collective-permute-start(f16[65,8,128]{2,1,0:T(8,128)(2,1)S(1)} %convert_element_type.96), channel_id=1, source_target_pairs={{0,2},{2,4},{4,6},{6,8},{8,10},{10,12},{12,14},{14,16},{16,18},{18... | collective-permute-start | bytes 399368 | tf_op jit(solution)/shard_map/ppermute | solution.py:320
  17.1 1.7 %propagate.13 = (f32[2,32,8,128]{3,2,1,0:T(8,128)S(1)}, f32[65,8,128]{2,1,0:T(8,128)S(1)}, f32[64,8,128]{2,1,0:T(8,128)S(1)}) custom-call(bf16[8,2,32,8,128]{4,3,2,1,0:T(8,128)(2,1)S(1)} %bitcast.21, bf16[8,2,32,8,128]{4,3,2,1,0:T(8,128)(2,1)S(1)} %collective-permute-done.refs_1_, f32[2,32,8,128]{3,2,1,0:T(8,128)S(1)} %pad_maximum_fusion.1.refs_2_, ...), custom_call_target="tpu_custom_call" | custom-call | tf_op jit(solution)/shard_map/jit(propagate)/propagate/pallas_call | solution.py:163
  18.9 2.8 %collective-permute-start.12 = (f16[65,8,128]{2,1,0:T(8,128)(2,1)S(1)}, f16[65,8,128]{2,1,0:T(8,128)(2,1)S(1)}, u32[]{:S(2)}, u32[]{:S(2)}) collective-permute-start(f16[65,8,128]{2,1,0:T(8,128)(2,1)S(1)} %convert_element_type.116), channel_id=1, source_target_pairs={{0,2},{2,4},{4,6},{6,8},{8,10},{10,12},{12,14},{14,16},{16,18},{18... | collective-permute-start | bytes 399368 | tf_op jit(solution)/shard_map/ppermute | solution.py:320
  23.0 3.2 %collective-permute-done.3 = f16[65,8,128]{2,1,0:T(8,128)(2,1)S(1)} collective-permute-done((f16[65,8,128]{2,1,0:T(8,128)(2,1)S(1)}, f16[65,8,128]{2,1,0:T(8,128)(2,1)S(1)}, u32[]{:S(2)}, u32[]{:S(2)}) %collective-permute-start.3) | collective-permute-done | bytes 133152 | tf_op jit(solution)/shard_map/ppermute | solution.py:320
  26.2 1.7 %propagate.9 = (f32[2,32,8,128]{3,2,1,0:T(8,128)S(1)}, f32[65,8,128]{2,1,0:T(8,128)S(1)}, f32[64,8,128]{2,1,0:T(8,128)S(1)}) custom-call(bf16[8,2,32,8,128]{4,3,2,1,0:T(8,128)(2,1)S(1)} %bitcast.22, bf16[8,2,32,8,128]{4,3,2,1,0:T(8,128)(2,1)S(1)} %collective-permute-done.refs_1_, f32[2,32,8,128]{3,2,1,0:T(8,128)S(1)} %pad_maximum_fusion.refs_2_, ...), custom_call_target="tpu_custom_call" | custom-call | tf_op jit(solution)/shard_map/jit(propagate)/propagate/pallas_call | solution.py:163
  27.9 1.3 %collective-permute-start.4 = (f16[65,8,128]{2,1,0:T(8,128)(2,1)S(1)}, f16[65,8,128]{2,1,0:T(8,128)(2,1)S(1)}, u32[]{:S(2)}, u32[]{:S(2)}) collective-permute-start(f16[65,8,128]{2,1,0:T(8,128)(2,1)S(1)} %convert_element_type.100), channel_id=1, source_target_pairs={{0,2},{2,4},{4,6},{6,8},{8,10},{10,12},{12,14},{14,16},{16,18},{18... | collective-permute-start | bytes 399368 | tf_op jit(solution)/shard_map/ppermute | solution.py:320
  30.6 1.5 %collective-permute-done.13 = f16[65,8,128]{2,1,0:T(8,128)(2,1)S(1)} collective-permute-done((f16[65,8,128]{2,1,0:T(8,128)(2,1)S(1)}, f16[65,8,128]{2,1,0:T(8,128)(2,1)S(1)}, u32[]{:S(2)}, u32[]{:S(2)}) %collective-permute-start.13) | collective-permute-done | bytes 133152 | tf_op jit(solution)/shard_map/ppermute | solution.py:320
  32.2 1.7 %propagate.14 = (f32[2,32,8,128]{3,2,1,0:T(8,128)S(1)}, f32[65,8,128]{2,1,0:T(8,128)S(1)}, f32[64,8,128]{2,1,0:T(8,128)S(1)}) custom-call(bf16[8,2,32,8,128]{4,3,2,1,0:T(8,128)(2,1)S(1)} %bitcast.24, bf16[8,2,32,8,128]{4,3,2,1,0:T(8,128)(2,1)S(1)} %collective-permute-done.refs_1_, f32[2,32,8,128]{3,2,1,0:T(8,128)S(1)} %get-tuple-element.73.refs_2_, ...), custom_call_target="tpu_custom_call" | custom-call | tf_op jit(solution)/shard_map/jit(propagate)/propagate/pallas_call | solution.py:163
  33.9 1.3 %collective-permute-start.14 = (f16[65,8,128]{2,1,0:T(8,128)(2,1)S(1)}, f16[65,8,128]{2,1,0:T(8,128)(2,1)S(1)}, u32[]{:S(2)}, u32[]{:S(2)}) collective-permute-start(f16[65,8,128]{2,1,0:T(8,128)(2,1)S(1)} %convert_element_type.120), channel_id=1, source_target_pairs={{0,2},{2,4},{4,6},{6,8},{8,10},{10,12},{12,14},{14,16},{16,18},{18... | collective-permute-start | bytes 399368 | tf_op jit(solution)/shard_map/ppermute | solution.py:320
  36.6 3.2 %collective-permute-done.5 = f16[65,8,128]{2,1,0:T(8,128)(2,1)S(1)} collective-permute-done((f16[65,8,128]{2,1,0:T(8,128)(2,1)S(1)}, f16[65,8,128]{2,1,0:T(8,128)(2,1)S(1)}, u32[]{:S(2)}, u32[]{:S(2)}) %collective-permute-start.5) | collective-permute-done | bytes 133152 | tf_op jit(solution)/shard_map/ppermute | solution.py:320
  39.8 1.7 %propagate.10 = (f32[2,32,8,128]{3,2,1,0:T(8,128)S(1)}, f32[65,8,128]{2,1,0:T(8,128)S(1)}, f32[64,8,128]{2,1,0:T(8,128)S(1)}) custom-call(bf16[8,2,32,8,128]{4,3,2,1,0:T(8,128)(2,1)S(1)} %bitcast.26, bf16[8,2,32,8,128]{4,3,2,1,0:T(8,128)(2,1)S(1)} %collective-permute-done.refs_1_, f32[2,32,8,128]{3,2,1,0:T(8,128)S(1)} %get-tuple-element.52.refs_2_, ...), custom_call_target="tpu_custom_call" | custom-call | tf_op jit(solution)/shard_map/jit(propagate)/propagate/pallas_call | solution.py:163
  41.5 1.3 %collective-permute-start.6 = (f16[65,8,128]{2,1,0:T(8,128)(2,1)S(1)}, f16[65,8,128]{2,1,0:T(8,128)(2,1)S(1)}, u32[]{:S(2)}, u32[]{:S(2)}) collective-permute-start(f16[65,8,128]{2,1,0:T(8,128)(2,1)S(1)} %convert_element_type.104), channel_id=1, source_target_pairs={{0,2},{2,4},{4,6},{6,8},{8,10},{10,12},{12,14},{14,16},{16,18},{18... | collective-permute-start | bytes 399368 | tf_op jit(solution)/shard_map/ppermute | solution.py:320
  45.8 1.7 %propagate.15 = (f32[2,32,8,128]{3,2,1,0:T(8,128)S(1)}, f32[65,8,128]{2,1,0:T(8,128)S(1)}) custom-call(bf16[8,2,32,8,128]{4,3,2,1,0:T(8,128)(2,1)S(1)} %bitcast.29, bf16[8,2,32,8,128]{4,3,2,1,0:T(8,128)(2,1)S(1)} %collective-permute-done.refs_1_, f32[2,32,8,128]{3,2,1,0:T(8,128)S(1)} %get-tuple-element.78.refs_2_, ...), custom_call_target="tpu_custom_call" | custom-call | tf_op jit(solution)/shard_map/jit(propagate)/propagate/pallas_call | solution.py:163
  47.5 1.3 %collective-permute-start.16 = (f16[65,8,128]{2,1,0:T(8,128)(2,1)S(1)}, f16[65,8,128]{2,1,0:T(8,128)(2,1)S(1)}, u32[]{:S(2)}, u32[]{:S(2)}) collective-permute-start(f16[65,8,128]{2,1,0:T(8,128)(2,1)S(1)} %convert_element_type.124), channel_id=1, source_target_pairs={{0,2},{2,4},{4,6},{6,8},{8,10},{10,12},{12,14},{14,16},{16,18},{18... | collective-permute-start | bytes 399368 | tf_op jit(solution)/shard_map/ppermute | solution.py:320
  50.2 4.3 %collective-permute-done.7 = f16[65,8,128]{2,1,0:T(8,128)(2,1)S(1)} collective-permute-done((f16[65,8,128]{2,1,0:T(8,128)(2,1)S(1)}, f16[65,8,128]{2,1,0:T(8,128)(2,1)S(1)}, u32[]{:S(2)}, u32[]{:S(2)}) %collective-permute-start.7) | collective-permute-done | bytes 133152 | tf_op jit(solution)/shard_map/ppermute | solution.py:320
  54.5 1.7 %propagate.11 = (f32[2,32,8,128]{3,2,1,0:T(8,128)S(1)}, f32[65,8,128]{2,1,0:T(8,128)S(1)}) custom-call(bf16[8,2,32,8,128]{4,3,2,1,0:T(8,128)(2,1)S(1)} %bitcast.31, bf16[8,2,32,8,128]{4,3,2,1,0:T(8,128)(2,1)S(1)} %collective-permute-done.refs_1_, f32[2,32,8,128]{3,2,1,0:T(8,128)S(1)} %get-tuple-element.57.refs_2_, ...), custom_call_target="tpu_custom_call" | custom-call | tf_op jit(solution)/shard_map/jit(propagate)/propagate/pallas_call | solution.py:163
  56.2 1.3 %collective-permute-start.8 = (f16[65,8,128]{2,1,0:T(8,128)(2,1)S(1)}, f16[65,8,128]{2,1,0:T(8,128)(2,1)S(1)}, u32[]{:S(2)}, u32[]{:S(2)}) collective-permute-start(f16[65,8,128]{2,1,0:T(8,128)(2,1)S(1)} %convert_element_type.108), channel_id=1, source_target_pairs={{0,2},{2,4},{4,6},{6,8},{8,10},{10,12},{12,14},{14,16},{16,18},{18... | collective-permute-start | bytes 399368 | tf_op jit(solution)/shard_map/ppermute | solution.py:320
  57.7 3.2 %collective-permute-done.9 = f16[65,8,128]{2,1,0:T(8,128)(2,1)S(1)} collective-permute-done((f16[65,8,128]{2,1,0:T(8,128)(2,1)S(1)}, f16[65,8,128]{2,1,0:T(8,128)(2,1)S(1)}, u32[]{:S(2)}, u32[]{:S(2)}) %collective-permute-start.9) | collective-permute-done | bytes 133152 | tf_op jit(solution)/shard_map/ppermute | solution.py:320
  61.1 1.3 %collective-permute-done.18.refs_2_ = f32[1,32,8,128]{3,2,1,0:T(8,128)S(1)} collective-permute-done((f32[1,32,8,128]{3,2,1,0:T(8,128)S(1)}, f32[1,32,8,128]{3,2,1,0:T(8,128)S(1)}, u32[]{:S(2)}, u32[]{:S(2)}) %collective-permute-start.18) | collective-permute-done | bytes 131104 | tf_op jit(solution)/shard_map/ppermute | solution.py:315
  62.6 12.8 %all_to_all.11 = f32[32,1,128]{2,1,0:T(1,128)S(1)} all-to-all(f32[32,1,128]{2,1,0:T(1,128)S(1)} %bitcast.33), channel_id=1, replica_groups=mesh['seg'=16,'slab'=2] {'seg','slab'}, dimensions={0} | all-to-all | bytes 32768 | tf_op jit(solution)/shard_map/all_to_all | solution.py:392
  (76 shorter events, 14.6 us)
Async XLA Ops:
  0.0 3.4 %copy-start = (bf16[1,8,2,8,4096]{4,3,2,1,0:T(8,128)(2,1)S(1)}, bf16[1,8,2,8,4096]{4,3,2,1,0:T(8,128)(2,1)}, u32[]{:S(2)}) copy-start(bf16[1,8,2,8,4096]{4,3,2,1,0:T(8,128)(2,1)} %param.3) | copy-start | bytes 3145732
  0.0 3.4 %collective-permute-start = (bf16[8,2,32,8,128]{4,3,2,1,0:T(8,128)(2,1)}, bf16[8,2,32,8,128]{4,3,2,1,0:T(8,128)(2,1)S(1)}, u32[]{:S(2)}, u32[]{:S(2)}) collective-permute-start(bf16[8,2,32,8,128]{4,3,2,1,0:T(8,128)(2,1)} %bitcast.15), channel_id=1, source_target_pairs={{1,0},{0,1},{3,2},{2,3},{5,4},{4,5},{7,6},{6,7},{9,8},{8,9},{11,10... | collective-permute-start | bytes 3145736 | tf_op jit(solution)/shard_map/ppermute | solution.py:315
  1.6 1.8 %collective-permute-start.1 = (f32[2,32,8,128]{3,2,1,0:T(8,128)S(1)}, f32[2,32,8,128]{3,2,1,0:T(8,128)S(1)}, u32[]{:S(2)}, u32[]{:S(2)}) collective-permute-start(f32[2,32,8,128]{3,2,1,0:T(8,128)S(1)} %get-tuple-element.94), channel_id=1, source_target_pairs={{1,0},{0,1},{3,2},{2,3},{5,4},{4,5},{7,6},{6,7},{9,8},{8,9},{11,10... | collective-permute-start | bytes 786440 | tf_op jit(solution)/shard_map/ppermute | solution.py:315
  3.4 13.7 %collective-permute-start.11 = (f16[65,8,128]{2,1,0:T(8,128)(2,1)S(1)}, f16[65,8,128]{2,1,0:T(8,128)(2,1)S(1)}, u32[]{:S(2)}, u32[]{:S(2)}) collective-permute-start(f16[65,8,128]{2,1,0:T(8,128)(2,1)S(1)} %convert_element_type.114), channel_id=1, source_target_pairs={{30,0},{31,1}} | collective-permute-start | bytes 399368 | tf_op jit(solution)/shard_map/ppermute | solution.py:320
  6.4 10.6 %collective-permute-start.10 = (f16[65,8,128]{2,1,0:T(8,128)(2,1)S(1)}, f16[65,8,128]{2,1,0:T(8,128)(2,1)S(1)}, u32[]{:S(2)}, u32[]{:S(2)}) collective-permute-start(f16[65,8,128]{2,1,0:T(8,128)(2,1)S(1)} %convert_element_type.112), channel_id=1, source_target_pairs={{0,2},{2,4},{4,6},{6,8},{8,10},{10,12},{12,14},{14,16},{16,18},{18... | collective-permute-start | bytes 399368 | tf_op jit(solution)/shard_map/ppermute | solution.py:320
  12.3 10.7 %collective-permute-start.2 = (f16[65,8,128]{2,1,0:T(8,128)(2,1)S(1)}, f16[65,8,128]{2,1,0:T(8,128)(2,1)S(1)}, u32[]{:S(2)}, u32[]{:S(2)}) collective-permute-start(f16[65,8,128]{2,1,0:T(8,128)(2,1)S(1)} %convert_element_type.96), channel_id=1, source_target_pairs={{0,2},{2,4},{4,6},{6,8},{8,10},{10,12},{12,14},{14,16},{16,18},{18... | collective-permute-start | bytes 399368 | tf_op jit(solution)/shard_map/ppermute | solution.py:320
  15.7 10.5 %collective-permute-start.3 = (f16[65,8,128]{2,1,0:T(8,128)(2,1)S(1)}, f16[65,8,128]{2,1,0:T(8,128)(2,1)S(1)}, u32[]{:S(2)}, u32[]{:S(2)}) collective-permute-start(f16[65,8,128]{2,1,0:T(8,128)(2,1)S(1)} %convert_element_type.98), channel_id=1, source_target_pairs={{30,0},{31,1}} | collective-permute-start | bytes 399368 | tf_op jit(solution)/shard_map/ppermute | solution.py:320
  18.9 11.7 %collective-permute-start.12 = (f16[65,8,128]{2,1,0:T(8,128)(2,1)S(1)}, f16[65,8,128]{2,1,0:T(8,128)(2,1)S(1)}, u32[]{:S(2)}, u32[]{:S(2)}) collective-permute-start(f16[65,8,128]{2,1,0:T(8,128)(2,1)S(1)} %convert_element_type.116), channel_id=1, source_target_pairs={{0,2},{2,4},{4,6},{6,8},{8,10},{10,12},{12,14},{14,16},{16,18},{18... | collective-permute-start | bytes 399368 | tf_op jit(solution)/shard_map/ppermute | solution.py:320
  21.7 10.5 %collective-permute-start.13 = (f16[65,8,128]{2,1,0:T(8,128)(2,1)S(1)}, f16[65,8,128]{2,1,0:T(8,128)(2,1)S(1)}, u32[]{:S(2)}, u32[]{:S(2)}) collective-permute-start(f16[65,8,128]{2,1,0:T(8,128)(2,1)S(1)} %convert_element_type.118), channel_id=1, source_target_pairs={{30,0},{31,1}} | collective-permute-start | bytes 399368 | tf_op jit(solution)/shard_map/ppermute | solution.py:320
  27.9 8.6 %collective-permute-start.4 = (f16[65,8,128]{2,1,0:T(8,128)(2,1)S(1)}, f16[65,8,128]{2,1,0:T(8,128)(2,1)S(1)}, u32[]{:S(2)}, u32[]{:S(2)}) collective-permute-start(f16[65,8,128]{2,1,0:T(8,128)(2,1)S(1)} %convert_element_type.100), channel_id=1, source_target_pairs={{0,2},{2,4},{4,6},{6,8},{8,10},{10,12},{12,14},{14,16},{16,18},{18... | collective-permute-start | bytes 399368 | tf_op jit(solution)/shard_map/ppermute | solution.py:320
  29.3 10.5 %collective-permute-start.5 = (f16[65,8,128]{2,1,0:T(8,128)(2,1)S(1)}, f16[65,8,128]{2,1,0:T(8,128)(2,1)S(1)}, u32[]{:S(2)}, u32[]{:S(2)}) collective-permute-start(f16[65,8,128]{2,1,0:T(8,128)(2,1)S(1)} %convert_element_type.102), channel_id=1, source_target_pairs={{30,0},{31,1}} | collective-permute-start | bytes 399368 | tf_op jit(solution)/shard_map/ppermute | solution.py:320
  33.9 10.3 %collective-permute-start.14 = (f16[65,8,128]{2,1,0:T(8,128)(2,1)S(1)}, f16[65,8,128]{2,1,0:T(8,128)(2,1)S(1)}, u32[]{:S(2)}, u32[]{:S(2)}) collective-permute-start(f16[65,8,128]{2,1,0:T(8,128)(2,1)S(1)} %convert_element_type.120), channel_id=1, source_target_pairs={{0,2},{2,4},{4,6},{6,8},{8,10},{10,12},{12,14},{14,16},{16,18},{18... | collective-permute-start | bytes 399368 | tf_op jit(solution)/shard_map/ppermute | solution.py:320
  35.3 10.5 %collective-permute-start.15 = (f16[65,8,128]{2,1,0:T(8,128)(2,1)S(1)}, f16[65,8,128]{2,1,0:T(8,128)(2,1)S(1)}, u32[]{:S(2)}, u32[]{:S(2)}) collective-permute-start(f16[65,8,128]{2,1,0:T(8,128)(2,1)S(1)} %convert_element_type.122), channel_id=1, source_target_pairs={{30,0},{31,1}} | collective-permute-start | bytes 399368 | tf_op jit(solution)/shard_map/ppermute | solution.py:320
  41.5 7.2 %collective-permute-start.6 = (f16[65,8,128]{2,1,0:T(8,128)(2,1)S(1)}, f16[65,8,128]{2,1,0:T(8,128)(2,1)S(1)}, u32[]{:S(2)}, u32[]{:S(2)}) collective-permute-start(f16[65,8,128]{2,1,0:T(8,128)(2,1)S(1)} %convert_element_type.104), channel_id=1, source_target_pairs={{0,2},{2,4},{4,6},{6,8},{8,10},{10,12},{12,14},{14,16},{16,18},{18... | collective-permute-start | bytes 399368 | tf_op jit(solution)/shard_map/ppermute | solution.py:320
  42.9 11.6 %collective-permute-start.7 = (f16[65,8,128]{2,1,0:T(8,128)(2,1)S(1)}, f16[65,8,128]{2,1,0:T(8,128)(2,1)S(1)}, u32[]{:S(2)}, u32[]{:S(2)}) collective-permute-start(f16[65,8,128]{2,1,0:T(8,128)(2,1)S(1)} %convert_element_type.106), channel_id=1, source_target_pairs={{30,0},{31,1}} | collective-permute-start | bytes 399368 | tf_op jit(solution)/shard_map/ppermute | solution.py:320
  44.3 13.2 %collective-permute-start.17 = (f16[65,8,128]{2,1,0:T(8,128)(2,1)S(1)}, f16[65,8,128]{2,1,0:T(8,128)(2,1)S(1)}, u32[]{:S(2)}, u32[]{:S(2)}) collective-permute-start(f16[65,8,128]{2,1,0:T(8,128)(2,1)S(1)} %convert_element_type.126), channel_id=1, source_target_pairs={{30,0},{31,1}} | collective-permute-start | bytes 399368 | tf_op jit(solution)/shard_map/ppermute | solution.py:320
  47.5 10.1 %collective-permute-start.16 = (f16[65,8,128]{2,1,0:T(8,128)(2,1)S(1)}, f16[65,8,128]{2,1,0:T(8,128)(2,1)S(1)}, u32[]{:S(2)}, u32[]{:S(2)}) collective-permute-start(f16[65,8,128]{2,1,0:T(8,128)(2,1)S(1)} %convert_element_type.124), channel_id=1, source_target_pairs={{0,2},{2,4},{4,6},{6,8},{8,10},{10,12},{12,14},{14,16},{16,18},{18... | collective-permute-start | bytes 399368 | tf_op jit(solution)/shard_map/ppermute | solution.py:320
  48.9 12.0 %collective-permute-start.9 = (f16[65,8,128]{2,1,0:T(8,128)(2,1)S(1)}, f16[65,8,128]{2,1,0:T(8,128)(2,1)S(1)}, u32[]{:S(2)}, u32[]{:S(2)}) collective-permute-start(f16[65,8,128]{2,1,0:T(8,128)(2,1)S(1)} %convert_element_type.110), channel_id=1, source_target_pairs={{30,0},{31,1}} | collective-permute-start | bytes 399368 | tf_op jit(solution)/shard_map/ppermute | solution.py:320
  56.2 4.7 %collective-permute-start.8 = (f16[65,8,128]{2,1,0:T(8,128)(2,1)S(1)}, f16[65,8,128]{2,1,0:T(8,128)(2,1)S(1)}, u32[]{:S(2)}, u32[]{:S(2)}) collective-permute-start(f16[65,8,128]{2,1,0:T(8,128)(2,1)S(1)} %convert_element_type.108), channel_id=1, source_target_pairs={{0,2},{2,4},{4,6},{6,8},{8,10},{10,12},{12,14},{14,16},{16,18},{18... | collective-permute-start | bytes 399368 | tf_op jit(solution)/shard_map/ppermute | solution.py:320
  57.6 3.4 %collective-permute-start.19 = (f32[1,32,8,128]{3,2,1,0:T(8,128)S(1)}, f32[1,32,8,128]{3,2,1,0:T(8,128)S(1)}, u32[]{:S(2)}, u32[]{:S(2)}) collective-permute-start(f32[1,32,8,128]{3,2,1,0:T(8,128)S(1)} %get-tuple-element.92), channel_id=1, source_target_pairs={{1,0},{0,1},{3,2},{2,3},{5,4},{4,5},{7,6},{6,7},{9,8},{8,9},{11,10... | collective-permute-start | bytes 393224 | tf_op jit(solution)/shard_map/ppermute | solution.py:315
  61.0 1.4 %collective-permute-start.18 = (f32[1,32,8,128]{3,2,1,0:T(8,128)S(1)}, f32[1,32,8,128]{3,2,1,0:T(8,128)S(1)}, u32[]{:S(2)}, u32[]{:S(2)}) collective-permute-start(f32[1,32,8,128]{3,2,1,0:T(8,128)S(1)} %get-tuple-element.91), channel_id=1, source_target_pairs={{1,0},{0,1},{3,2},{2,3},{5,4},{4,5},{7,6},{6,7},{9,8},{8,9},{11,10... | collective-permute-start | bytes 393224 | tf_op jit(solution)/shard_map/ppermute | solution.py:315
where the time goes:
time: 76.9 us; the launch traced here: 76.5 us
  starting transfers between devices  27.9 us (36%)
  waiting for transfers between devices  18.4 us (24%)
  Pallas kernels  14.9 us (19%)
  blocking collectives  12.8 us (17%)
  local copies, waits for them, and re-layouts  1.1 us (1%)
    ppermute x16, starting transfers between devices, to_next(): lax.ppermute(value, 'seg', [(i, (i + 1) % size) for i in segments or rang...  27.1 us
    ppermute x16, waiting for transfers between devices, to_next(): lax.ppermute(value, 'seg', [(i, (i + 1) % size) for i in segments or rang...  15.5 us
    pallas_call x16, Pallas kernels, propagate(): pl.pallas_call(functools.partial(propagate_kernel, pieces, index, first,...  13.5 us
    all_to_all x1, blocking collectives, shards(): gram = lax.all_to_all(gram, axes, 0, 0, tiled=True)  12.8 us
    ppermute x4, waiting for transfers between devices, from_slab(): lax.ppermute(value, 'slab', [((i + distance) % size, i) for i in range(si...  2.95 us
  transfers between devices with their start and end apart: 20, of which 8 were waited for; matrix products, arithmetic and copies ran while one was open for 2% of the time, Pallas kernels for 18%

commit v1 on v0

--- a/solution.py
+++ b/solution.py
@@ -90,9 +90,17 @@
         pl.when(chosen)(functools.partial(run, message, previous))
 
 
-def ends_of_ring():
-    here = lax.axis_index("seg")
-    return here == lax.axis_size("seg") - 1, here == 0
+GROUP = 4
+
+
+def group_size(segments):
+    return GROUP if segments % GROUP == 0 else segments
+
+
+def ends_of_group():
+    group = group_size(lax.axis_size("seg"))
+    place = lax.rem(lax.axis_index("seg"), group)
+    return place == group - 1, place == 0
 
 
 def propagate_kernel(pieces, index, first, last, final, *refs):
@@ -110,7 +118,7 @@
     (sent,) = take(1)
     error = None if final else take(1)[0]
     ping, pong = refs
-    at_last, at_first = ends_of_ring()
+    at_last, at_first = ends_of_group()
 
     @pl.when(at_last if last else jnp.logical_not(at_last))
     def _():
@@ -175,7 +183,7 @@
     def use(piece, j, at, b, value):
         outs[piece][0, j, at, :] = value
 
-    at_last, at_first = ends_of_ring()
+    at_last, at_first = ends_of_group()
     rest = jnp.logical_not(jnp.logical_or(at_last, at_first))
     cases = [(at_last, message, previous_last), (at_first, wrapped, previous), (rest, message, previous)]
     take_in(cases, use)
@@ -315,13 +323,27 @@
     return lax.ppermute(value, "slab", [((i + distance) % size, i) for i in range(size)])
 
 
-def to_next(value, segments=None):
+def to_next(value):
     size = lax.axis_size("seg")
-    return lax.ppermute(value, "seg", [(i, (i + 1) % size) for i in segments or range(size)])
-
-
-def sent_short(message, segments=None):
-    return to_next(message.astype(jnp.float16), segments).astype(jnp.float32)
+    return lax.ppermute(value, "seg", [(i, (i + 1) % size) for i in range(size)])
+
+
+def within_group(message):
+    size = lax.axis_size("seg")
+    group = group_size(size)
+    route = [(i, i + 1 if (i + 1) % group else i + 1 - group) for i in range(size)]
+    return lax.ppermute(message.astype(jnp.float16), "seg", route).astype(jnp.float32)
+
+
+def to_next_group(message):
+    size = lax.axis_size("seg")
+    group = group_size(size)
+    route = []
+    for i in range(size):
+        place = i % group
+        target = (i + 1) % size if place == group - 1 else i + group - 1 if place == 0 else i
+        route.append((i, target))
+    return lax.ppermute(message.astype(jnp.float16), "seg", route).astype(jnp.float32)
 
 
 def split_vectors(vectors, velocity):
@@ -336,7 +358,6 @@
     for d in range(1, slabs):
         start.append(from_slab(part(slabs - d), d))
         speeds.append(from_slab(velocity, d))
-    end = lax.axis_size("seg") - 1
     previous = [jnp.concatenate([part[i : i + 1] for part in start], 0) for i in range(share)]
     own, ends = list(previous), list(previous)
     arrived, wrapped, missed, missed_end = [[None] * share for _ in range(4)]
@@ -355,8 +376,8 @@
             if not final:
                 missed_end[i], missed[i] = out_end.pop(), out.pop()
             sent_end, sent = out_end[0], out[0]
-            wrapped[i] = sent_short(sent_end, [end])
-            arrived[i] = sent_short(sent, range(end))
+            wrapped[i] = to_next_group(sent_end)
+            arrived[i] = within_group(sent)
     parts = [last_residual(arrived[i], wrapped[i], own[i], ends[i]) for i in range(share)]
     residual = []
     for d in range(slabs):

time: 76.9 us -> 85.5 us (1.11)
  starting transfers between devices: 27.9 us -> 47.7 us
  waiting for transfers between devices: 18.4 us -> 9.99 us
  blocking collectives: 12.8 us -> 10.1 us
    ppermute x16, starting transfers between devices: 27.1 us -> 46.9 us  [the longest x8 46.4 us: to_next_group(): lax.ppermute(message.astype(jnp.float16), 'seg', route).astype(jnp.float32)]
    ppermute x16, waiting for transfers between devices: 15.5 us -> 7.05 us  [the longest x8 3.83 us: within_group(): lax.ppermute(message.astype(jnp.float16), 'seg', route).astype(jnp.float32)]
    all_to_all x1, blocking collectives: 12.8 us -> 10.1 us  [shards(): gram = lax.all_to_all(gram, axes, 0, 0, tiled=True)]
  transfers between devices with their start and end apart: 20 -> 20, of which waited for: 8 -> 5; matrix products, arithmetic and copies ran while one was open for 2% -> 2% of each run, Pallas kernels for 18% -> 16%
where the time goes in v1:
time: 85.5 us; the launch traced here: 85.1 us
  starting transfers between devices  47.7 us (56%)
  Pallas kernels  14.9 us (17%)
  blocking collectives  10.1 us (12%)
  waiting for transfers between devices  9.99 us (12%)
  local copies, waits for them, and re-layouts  1.1 us (1%)
    ppermute x8, starting transfers between devices, to_next_group(): lax.ppermute(message.astype(jnp.float16), 'seg', route).astype(jnp.float32)  46.4 us
    pallas_call x16, Pallas kernels, propagate(): pl.pallas_call(functools.partial(propagate_kernel, pieces, index, first,...  13.5 us
    all_to_all x1, blocking collectives, shards(): gram = lax.all_to_all(gram, axes, 0, 0, tiled=True)  10.1 us
    ppermute x8, waiting for transfers between devices, within_group(): lax.ppermute(message.astype(jnp.float16), 'seg', route).astype(jnp.float32)  3.83 us
    ppermute x8, waiting for transfers between devices, to_next_group(): lax.ppermute(message.astype(jnp.float16), 'seg', route).astype(jnp.float32)  3.21 us
    ppermute x4, waiting for transfers between devices, from_slab(): lax.ppermute(value, 'slab', [((i + distance) % size, i) for i in range(si...  2.95 us
  transfers between devices with their start and end apart: 20, of which 5 were waited for; matrix products, arithmetic and copies ran while one was open for 2% of the time, Pallas kernels for 16%

profile of v1, /device:TPU:0, one launch (start us, length us, event | category | flops | bytes accessed | tf_op | source)
XLA Modules:
  0.0 85.1 jit_solution(4936434171858886098)
XLA Ops:
  0.5 1.1 %dynamic-slice_bitcast_fusion.1 = (f32[2,32,8,128]{3,2,1,0:T(8,128)S(1)}, f32[2,32,8,128]{3,2,1,0:T(8,128)S(1)}) fusion(f32[4,8,32,128]{3,1,2,0:T(8,128)} %bitcast.34, s32[]{:T(128)S(6)} %select_n.6, s32[]{:T(128)S(6)} %select_n.7), kind=kLoop, calls=%fused_computation.3 | loop fusion | bytes 1048584 | tf_op jit(solution)/shard_map/dynamic_slice | solution.py:355
  1.8 1.6 %collective-permute-done.1.refs_3_ = f32[2,32,8,128]{3,2,1,0:T(8,128)S(1)} collective-permute-done((f32[2,32,8,128]{3,2,1,0:T(8,128)S(1)}, f32[2,32,8,128]{3,2,1,0:T(8,128)S(1)}, u32[]{:S(2)}, u32[]{:S(2)}) %collective-permute-start.1) | collective-permute-done | bytes 262176 | tf_op jit(solution)/shard_map/ppermute | solution.py:323
  3.4 7.4 %collective-permute-start.11 = (f16[65,8,128]{2,1,0:T(8,128)(2,1)S(1)}, f16[65,8,128]{2,1,0:T(8,128)(2,1)S(1)}, u32[]{:S(2)}, u32[]{:S(2)}) collective-permute-start(f16[65,8,128]{2,1,0:T(8,128)(2,1)S(1)} %convert_element_type.114), channel_id=1, source_target_pairs={{0,6},{2,2},{4,4},{6,8},{8,14},{10,10},{12,12},{14,16},{16,22},{18... | collective-permute-start | bytes 399368 | tf_op jit(solution)/shard_map/ppermute | solution.py:346
  10.8 1.6 %propagate.12 = (f32[65,8,128]{2,1,0:T(8,128)S(1)}, f32[64,8,128]{2,1,0:T(8,128)S(1)}) custom-call(bf16[8,2,32,8,128]{4,3,2,1,0:T(8,128)(2,1)S(1)} %bitcast.17, bf16[8,2,32,8,128]{4,3,2,1,0:T(8,128)(2,1)S(1)} %collective-permute-done.refs_1_, f32[2,32,8,128]{3,2,1,0:T(8,128)S(1)} %get-tuple-element.93.refs_2_, ...), custom_call_target="tpu_custom_call" | custom-call | tf_op jit(solution)/shard_map/jit(propagate)/propagate/pallas_call | solution.py:171
  12.6 1.6 %propagate.8 = (f32[65,8,128]{2,1,0:T(8,128)S(1)}, f32[64,8,128]{2,1,0:T(8,128)S(1)}) custom-call(bf16[8,2,32,8,128]{4,3,2,1,0:T(8,128)(2,1)S(1)} %bitcast.19, bf16[8,2,32,8,128]{4,3,2,1,0:T(8,128)(2,1)S(1)} %collective-permute-done.refs_1_, f32[2,32,8,128]{3,2,1,0:T(8,128)S(1)} %get-tuple-element.93.refs_2_, ...), custom_call_target="tpu_custom_call" | custom-call | tf_op jit(solution)/shard_map/jit(propagate)/propagate/pallas_call | solution.py:171
  14.3 4.8 %collective-permute-start.3 = (f16[65,8,128]{2,1,0:T(8,128)(2,1)S(1)}, f16[65,8,128]{2,1,0:T(8,128)(2,1)S(1)}, u32[]{:S(2)}, u32[]{:S(2)}) collective-permute-start(f16[65,8,128]{2,1,0:T(8,128)(2,1)S(1)} %convert_element_type.98), channel_id=1, source_target_pairs={{0,6},{2,2},{4,4},{6,8},{8,14},{10,10},{12,12},{14,16},{16,22},{18... | collective-permute-start | bytes 399368 | tf_op jit(solution)/shard_map/ppermute | solution.py:346
  19.2 1.4 %collective-permute-done.10 = f16[65,8,128]{2,1,0:T(8,128)(2,1)S(1)} collective-permute-done((f16[65,8,128]{2,1,0:T(8,128)(2,1)S(1)}, f16[65,8,128]{2,1,0:T(8,128)(2,1)S(1)}, u32[]{:S(2)}, u32[]{:S(2)}) %collective-permute-start.10) | collective-permute-done | bytes 133152 | tf_op jit(solution)/shard_map/ppermute | solution.py:335
  20.7 1.7 %propagate.13 = (f32[2,32,8,128]{3,2,1,0:T(8,128)S(1)}, f32[65,8,128]{2,1,0:T(8,128)S(1)}, f32[64,8,128]{2,1,0:T(8,128)S(1)}) custom-call(bf16[8,2,32,8,128]{4,3,2,1,0:T(8,128)(2,1)S(1)} %bitcast.21, bf16[8,2,32,8,128]{4,3,2,1,0:T(8,128)(2,1)S(1)} %collective-permute-done.refs_1_, f32[2,32,8,128]{3,2,1,0:T(8,128)S(1)} %pad_maximum_fusion.1.refs_2_, ...), custom_call_target="tpu_custom_call" | custom-call | tf_op jit(solution)/shard_map/jit(propagate)/propagate/pallas_call | solution.py:171
  22.5 4.8 %collective-permute-start.13 = (f16[65,8,128]{2,1,0:T(8,128)(2,1)S(1)}, f16[65,8,128]{2,1,0:T(8,128)(2,1)S(1)}, u32[]{:S(2)}, u32[]{:S(2)}) collective-permute-start(f16[65,8,128]{2,1,0:T(8,128)(2,1)S(1)} %convert_element_type.118), channel_id=1, source_target_pairs={{0,6},{2,2},{4,4},{6,8},{8,14},{10,10},{12,12},{14,16},{16,22},{18... | collective-permute-start | bytes 399368 | tf_op jit(solution)/shard_map/ppermute | solution.py:346
  27.4 1.7 %propagate.9 = (f32[2,32,8,128]{3,2,1,0:T(8,128)S(1)}, f32[65,8,128]{2,1,0:T(8,128)S(1)}, f32[64,8,128]{2,1,0:T(8,128)S(1)}) custom-call(bf16[8,2,32,8,128]{4,3,2,1,0:T(8,128)(2,1)S(1)} %bitcast.22, bf16[8,2,32,8,128]{4,3,2,1,0:T(8,128)(2,1)S(1)} %collective-permute-done.refs_1_, f32[2,32,8,128]{3,2,1,0:T(8,128)S(1)} %pad_maximum_fusion.refs_2_, ...), custom_call_target="tpu_custom_call" | custom-call | tf_op jit(solution)/shard_map/jit(propagate)/propagate/pallas_call | solution.py:171
  29.2 6.5 %collective-permute-start.5 = (f16[65,8,128]{2,1,0:T(8,128)(2,1)S(1)}, f16[65,8,128]{2,1,0:T(8,128)(2,1)S(1)}, u32[]{:S(2)}, u32[]{:S(2)}) collective-permute-start(f16[65,8,128]{2,1,0:T(8,128)(2,1)S(1)} %convert_element_type.102), channel_id=1, source_target_pairs={{0,6},{2,2},{4,4},{6,8},{8,14},{10,10},{12,12},{14,16},{16,22},{18... | collective-permute-start | bytes 399368 | tf_op jit(solution)/shard_map/ppermute | solution.py:346
  35.8 1.7 %propagate.14 = (f32[2,32,8,128]{3,2,1,0:T(8,128)S(1)}, f32[65,8,128]{2,1,0:T(8,128)S(1)}, f32[64,8,128]{2,1,0:T(8,128)S(1)}) custom-call(bf16[8,2,32,8,128]{4,3,2,1,0:T(8,128)(2,1)S(1)} %bitcast.24, bf16[8,2,32,8,128]{4,3,2,1,0:T(8,128)(2,1)S(1)} %collective-permute-done.refs_1_, f32[2,32,8,128]{3,2,1,0:T(8,128)S(1)} %get-tuple-element.73.refs_2_, ...), custom_call_target="tpu_custom_call" | custom-call | tf_op jit(solution)/shard_map/jit(propagate)/propagate/pallas_call | solution.py:171
  37.7 6.5 %collective-permute-start.15 = (f16[65,8,128]{2,1,0:T(8,128)(2,1)S(1)}, f16[65,8,128]{2,1,0:T(8,128)(2,1)S(1)}, u32[]{:S(2)}, u32[]{:S(2)}) collective-permute-start(f16[65,8,128]{2,1,0:T(8,128)(2,1)S(1)} %convert_element_type.122), channel_id=1, source_target_pairs={{0,6},{2,2},{4,4},{6,8},{8,14},{10,10},{12,12},{14,16},{16,22},{18... | collective-permute-start | bytes 399368 | tf_op jit(solution)/shard_map/ppermute | solution.py:346
  44.2 1.7 %propagate.10 = (f32[2,32,8,128]{3,2,1,0:T(8,128)S(1)}, f32[65,8,128]{2,1,0:T(8,128)S(1)}, f32[64,8,128]{2,1,0:T(8,128)S(1)}) custom-call(bf16[8,2,32,8,128]{4,3,2,1,0:T(8,128)(2,1)S(1)} %bitcast.26, bf16[8,2,32,8,128]{4,3,2,1,0:T(8,128)(2,1)S(1)} %collective-permute-done.refs_1_, f32[2,32,8,128]{3,2,1,0:T(8,128)S(1)} %get-tuple-element.52.refs_2_, ...), custom_call_target="tpu_custom_call" | custom-call | tf_op jit(solution)/shard_map/jit(propagate)/propagate/pallas_call | solution.py:171
  46.1 6.5 %collective-permute-start.7 = (f16[65,8,128]{2,1,0:T(8,128)(2,1)S(1)}, f16[65,8,128]{2,1,0:T(8,128)(2,1)S(1)}, u32[]{:S(2)}, u32[]{:S(2)}) collective-permute-start(f16[65,8,128]{2,1,0:T(8,128)(2,1)S(1)} %convert_element_type.106), channel_id=1, source_target_pairs={{0,6},{2,2},{4,4},{6,8},{8,14},{10,10},{12,12},{14,16},{16,22},{18... | collective-permute-start | bytes 399368 | tf_op jit(solution)/shard_map/ppermute | solution.py:346
  52.6 3.6 %collective-permute-start.17 = (f16[65,8,128]{2,1,0:T(8,128)(2,1)S(1)}, f16[65,8,128]{2,1,0:T(8,128)(2,1)S(1)}, u32[]{:S(2)}, u32[]{:S(2)}) collective-permute-start(f16[65,8,128]{2,1,0:T(8,128)(2,1)S(1)} %convert_element_type.126), channel_id=1, source_target_pairs={{0,6},{2,2},{4,4},{6,8},{8,14},{10,10},{12,12},{14,16},{16,22},{18... | collective-permute-start | bytes 399368 | tf_op jit(solution)/shard_map/ppermute | solution.py:346
  56.3 1.7 %propagate.15 = (f32[2,32,8,128]{3,2,1,0:T(8,128)S(1)}, f32[65,8,128]{2,1,0:T(8,128)S(1)}) custom-call(bf16[8,2,32,8,128]{4,3,2,1,0:T(8,128)(2,1)S(1)} %bitcast.29, bf16[8,2,32,8,128]{4,3,2,1,0:T(8,128)(2,1)S(1)} %collective-permute-done.refs_1_, f32[2,32,8,128]{3,2,1,0:T(8,128)S(1)} %get-tuple-element.78.refs_2_, ...), custom_call_target="tpu_custom_call" | custom-call | tf_op jit(solution)/shard_map/jit(propagate)/propagate/pallas_call | solution.py:171
  58.1 6.5 %collective-permute-start.9 = (f16[65,8,128]{2,1,0:T(8,128)(2,1)S(1)}, f16[65,8,128]{2,1,0:T(8,128)(2,1)S(1)}, u32[]{:S(2)}, u32[]{:S(2)}) collective-permute-start(f16[65,8,128]{2,1,0:T(8,128)(2,1)S(1)} %convert_element_type.110), channel_id=1, source_target_pairs={{0,6},{2,2},{4,4},{6,8},{8,14},{10,10},{12,12},{14,16},{16,22},{18... | collective-permute-start | bytes 399368 | tf_op jit(solution)/shard_map/ppermute | solution.py:346
  64.6 1.7 %propagate.11 = (f32[2,32,8,128]{3,2,1,0:T(8,128)S(1)}, f32[65,8,128]{2,1,0:T(8,128)S(1)}) custom-call(bf16[8,2,32,8,128]{4,3,2,1,0:T(8,128)(2,1)S(1)} %bitcast.31, bf16[8,2,32,8,128]{4,3,2,1,0:T(8,128)(2,1)S(1)} %collective-permute-done.refs_1_, f32[2,32,8,128]{3,2,1,0:T(8,128)S(1)} %get-tuple-element.57.refs_2_, ...), custom_call_target="tpu_custom_call" | custom-call | tf_op jit(solution)/shard_map/jit(propagate)/propagate/pallas_call | solution.py:171
  66.6 3.2 %collective-permute-done.9 = f16[65,8,128]{2,1,0:T(8,128)(2,1)S(1)} collective-permute-done((f16[65,8,128]{2,1,0:T(8,128)(2,1)S(1)}, f16[65,8,128]{2,1,0:T(8,128)(2,1)S(1)}, u32[]{:S(2)}, u32[]{:S(2)}) %collective-permute-start.9) | collective-permute-done | bytes 133152 | tf_op jit(solution)/shard_map/ppermute | solution.py:346
  69.9 2.4 %collective-permute-done.8 = f16[65,8,128]{2,1,0:T(8,128)(2,1)S(1)} collective-permute-done((f16[65,8,128]{2,1,0:T(8,128)(2,1)S(1)}, f16[65,8,128]{2,1,0:T(8,128)(2,1)S(1)}, u32[]{:S(2)}, u32[]{:S(2)}) %collective-permute-start.8) | collective-permute-done | bytes 133152 | tf_op jit(solution)/shard_map/ppermute | solution.py:335
  72.5 1.3 %collective-permute-done.18.refs_2_ = f32[1,32,8,128]{3,2,1,0:T(8,128)S(1)} collective-permute-done((f32[1,32,8,128]{3,2,1,0:T(8,128)S(1)}, f32[1,32,8,128]{3,2,1,0:T(8,128)S(1)}, u32[]{:S(2)}, u32[]{:S(2)}) %collective-permute-start.18) | collective-permute-done | bytes 131104 | tf_op jit(solution)/shard_map/ppermute | solution.py:323
  74.0 10.1 %all_to_all.11 = f32[32,1,128]{2,1,0:T(1,128)S(1)} all-to-all(f32[32,1,128]{2,1,0:T(1,128)S(1)} %bitcast.33), channel_id=1, replica_groups=mesh['seg'=16,'slab'=2] {'seg','slab'}, dimensions={0} | all-to-all | bytes 32768 | tf_op jit(solution)/shard_map/all_to_all | solution.py:413
  84.1 1.1 %solve.1 = f32[4,32,8,128]{3,2,1,0:T(8,128)} custom-call(f32[32,128]{1,0:T(8,128)S(1)} %bitcast.32, f32[1,32,8,128]{3,2,1,0:T(8,128)S(1)} %get-tuple-element.69.refs_0_, f32[1,32,8,128]{3,2,1,0:T(8,128)S(1)} %get-tuple-element.90.refs_1_, f32[1,32,8,128]{3,2,1,0:T(8,128)S(1)} %collective-permute-done.18.refs_2_, ...), custom_call_target="tpu_custom_call" | custom-call | tf_op jit(solution)/shard_map/solve/pallas_call | solution.py:311
  (76 shorter events, 2.5 us)
Async XLA Ops:
  0.0 3.4 %copy-start = (bf16[1,8,2,8,4096]{4,3,2,1,0:T(8,128)(2,1)S(1)}, bf16[1,8,2,8,4096]{4,3,2,1,0:T(8,128)(2,1)}, u32[]{:S(2)}) copy-start(bf16[1,8,2,8,4096]{4,3,2,1,0:T(8,128)(2,1)} %param.3) | copy-start | bytes 3145732
  0.0 3.4 %collective-permute-start = (bf16[8,2,32,8,128]{4,3,2,1,0:T(8,128)(2,1)}, bf16[8,2,32,8,128]{4,3,2,1,0:T(8,128)(2,1)S(1)}, u32[]{:S(2)}, u32[]{:S(2)}) collective-permute-start(bf16[8,2,32,8,128]{4,3,2,1,0:T(8,128)(2,1)} %bitcast.15), channel_id=1, source_target_pairs={{1,0},{0,1},{3,2},{2,3},{5,4},{4,5},{7,6},{6,7},{9,8},{8,9},{11,10... | collective-permute-start | bytes 3145736 | tf_op jit(solution)/shard_map/ppermute | solution.py:323
  1.6 1.8 %collective-permute-start.1 = (f32[2,32,8,128]{3,2,1,0:T(8,128)S(1)}, f32[2,32,8,128]{3,2,1,0:T(8,128)S(1)}, u32[]{:S(2)}, u32[]{:S(2)}) collective-permute-start(f32[2,32,8,128]{3,2,1,0:T(8,128)S(1)} %get-tuple-element.94), channel_id=1, source_target_pairs={{1,0},{0,1},{3,2},{2,3},{5,4},{4,5},{7,6},{6,7},{9,8},{8,9},{11,10... | collective-permute-start | bytes 786440 | tf_op jit(solution)/shard_map/ppermute | solution.py:323
  3.4 17.3 %collective-permute-start.11 = (f16[65,8,128]{2,1,0:T(8,128)(2,1)S(1)}, f16[65,8,128]{2,1,0:T(8,128)(2,1)S(1)}, u32[]{:S(2)}, u32[]{:S(2)}) collective-permute-start(f16[65,8,128]{2,1,0:T(8,128)(2,1)S(1)} %convert_element_type.114), channel_id=1, source_target_pairs={{0,6},{2,2},{4,4},{6,8},{8,14},{10,10},{12,12},{14,16},{16,22},{18... | collective-permute-start | bytes 399368 | tf_op jit(solution)/shard_map/ppermute | solution.py:346
  12.4 8.1 %collective-permute-start.10 = (f16[65,8,128]{2,1,0:T(8,128)(2,1)S(1)}, f16[65,8,128]{2,1,0:T(8,128)(2,1)S(1)}, u32[]{:S(2)}, u32[]{:S(2)}) collective-permute-start(f16[65,8,128]{2,1,0:T(8,128)(2,1)S(1)} %convert_element_type.112), channel_id=1, source_target_pairs={{0,2},{2,4},{4,6},{6,0},{8,10},{10,12},{12,14},{14,8},{16,18},{18,... | collective-permute-start | bytes 399368 | tf_op jit(solution)/shard_map/ppermute | solution.py:335
  14.3 13.1 %collective-permute-start.2 = (f16[65,8,128]{2,1,0:T(8,128)(2,1)S(1)}, f16[65,8,128]{2,1,0:T(8,128)(2,1)S(1)}, u32[]{:S(2)}, u32[]{:S(2)}) collective-permute-start(f16[65,8,128]{2,1,0:T(8,128)(2,1)S(1)} %convert_element_type.96), channel_id=1, source_target_pairs={{0,2},{2,4},{4,6},{6,0},{8,10},{10,12},{12,14},{14,8},{16,18},{18,... | collective-permute-start | bytes 399368 | tf_op jit(solution)/shard_map/ppermute | solution.py:335
  14.3 13.0 %collective-permute-start.3 = (f16[65,8,128]{2,1,0:T(8,128)(2,1)S(1)}, f16[65,8,128]{2,1,0:T(8,128)(2,1)S(1)}, u32[]{:S(2)}, u32[]{:S(2)}) collective-permute-start(f16[65,8,128]{2,1,0:T(8,128)(2,1)S(1)} %convert_element_type.98), channel_id=1, source_target_pairs={{0,6},{2,2},{4,4},{6,8},{8,14},{10,10},{12,12},{14,16},{16,22},{18... | collective-permute-start | bytes 399368 | tf_op jit(solution)/shard_map/ppermute | solution.py:346
  22.4 13.3 %collective-permute-start.12 = (f16[65,8,128]{2,1,0:T(8,128)(2,1)S(1)}, f16[65,8,128]{2,1,0:T(8,128)(2,1)S(1)}, u32[]{:S(2)}, u32[]{:S(2)}) collective-permute-start(f16[65,8,128]{2,1,0:T(8,128)(2,1)S(1)} %convert_element_type.116), channel_id=1, source_target_pairs={{0,2},{2,4},{4,6},{6,0},{8,10},{10,12},{12,14},{14,8},{16,18},{18,... | collective-permute-start | bytes 399368 | tf_op jit(solution)/shard_map/ppermute | solution.py:335
  22.5 13.3 %collective-permute-start.13 = (f16[65,8,128]{2,1,0:T(8,128)(2,1)S(1)}, f16[65,8,128]{2,1,0:T(8,128)(2,1)S(1)}, u32[]{:S(2)}, u32[]{:S(2)}) collective-permute-start(f16[65,8,128]{2,1,0:T(8,128)(2,1)S(1)} %convert_element_type.118), channel_id=1, source_target_pairs={{0,6},{2,2},{4,4},{6,8},{8,14},{10,10},{12,12},{14,16},{16,22},{18... | collective-permute-start | bytes 399368 | tf_op jit(solution)/shard_map/ppermute | solution.py:346
  29.1 15.0 %collective-permute-start.4 = (f16[65,8,128]{2,1,0:T(8,128)(2,1)S(1)}, f16[65,8,128]{2,1,0:T(8,128)(2,1)S(1)}, u32[]{:S(2)}, u32[]{:S(2)}) collective-permute-start(f16[65,8,128]{2,1,0:T(8,128)(2,1)S(1)} %convert_element_type.100), channel_id=1, source_target_pairs={{0,2},{2,4},{4,6},{6,0},{8,10},{10,12},{12,14},{14,8},{16,18},{18,... | collective-permute-start | bytes 399368 | tf_op jit(solution)/shard_map/ppermute | solution.py:335
  29.2 14.9 %collective-permute-start.5 = (f16[65,8,128]{2,1,0:T(8,128)(2,1)S(1)}, f16[65,8,128]{2,1,0:T(8,128)(2,1)S(1)}, u32[]{:S(2)}, u32[]{:S(2)}) collective-permute-start(f16[65,8,128]{2,1,0:T(8,128)(2,1)S(1)} %convert_element_type.102), channel_id=1, source_target_pairs={{0,6},{2,2},{4,4},{6,8},{8,14},{10,10},{12,12},{14,16},{16,22},{18... | collective-permute-start | bytes 399368 | tf_op jit(solution)/shard_map/ppermute | solution.py:346
  37.5 15.0 %collective-permute-start.14 = (f16[65,8,128]{2,1,0:T(8,128)(2,1)S(1)}, f16[65,8,128]{2,1,0:T(8,128)(2,1)S(1)}, u32[]{:S(2)}, u32[]{:S(2)}) collective-permute-start(f16[65,8,128]{2,1,0:T(8,128)(2,1)S(1)} %convert_element_type.120), channel_id=1, source_target_pairs={{0,2},{2,4},{4,6},{6,0},{8,10},{10,12},{12,14},{14,8},{16,18},{18,... | collective-permute-start | bytes 399368 | tf_op jit(solution)/shard_map/ppermute | solution.py:335
  37.7 18.6 %collective-permute-start.15 = (f16[65,8,128]{2,1,0:T(8,128)(2,1)S(1)}, f16[65,8,128]{2,1,0:T(8,128)(2,1)S(1)}, u32[]{:S(2)}, u32[]{:S(2)}) collective-permute-start(f16[65,8,128]{2,1,0:T(8,128)(2,1)S(1)} %convert_element_type.122), channel_id=1, source_target_pairs={{0,6},{2,2},{4,4},{6,8},{8,14},{10,10},{12,12},{14,16},{16,22},{18... | collective-permute-start | bytes 399368 | tf_op jit(solution)/shard_map/ppermute | solution.py:346
  45.9 12.1 %collective-permute-start.6 = (f16[65,8,128]{2,1,0:T(8,128)(2,1)S(1)}, f16[65,8,128]{2,1,0:T(8,128)(2,1)S(1)}, u32[]{:S(2)}, u32[]{:S(2)}) collective-permute-start(f16[65,8,128]{2,1,0:T(8,128)(2,1)S(1)} %convert_element_type.104), channel_id=1, source_target_pairs={{0,2},{2,4},{4,6},{6,0},{8,10},{10,12},{12,14},{14,8},{16,18},{18,... | collective-permute-start | bytes 399368 | tf_op jit(solution)/shard_map/ppermute | solution.py:335
  46.1 18.5 %collective-permute-start.7 = (f16[65,8,128]{2,1,0:T(8,128)(2,1)S(1)}, f16[65,8,128]{2,1,0:T(8,128)(2,1)S(1)}, u32[]{:S(2)}, u32[]{:S(2)}) collective-permute-start(f16[65,8,128]{2,1,0:T(8,128)(2,1)S(1)} %convert_element_type.106), channel_id=1, source_target_pairs={{0,6},{2,2},{4,4},{6,8},{8,14},{10,10},{12,12},{14,16},{16,22},{18... | collective-permute-start | bytes 399368 | tf_op jit(solution)/shard_map/ppermute | solution.py:346
  52.6 13.8 %collective-permute-start.17 = (f16[65,8,128]{2,1,0:T(8,128)(2,1)S(1)}, f16[65,8,128]{2,1,0:T(8,128)(2,1)S(1)}, u32[]{:S(2)}, u32[]{:S(2)}) collective-permute-start(f16[65,8,128]{2,1,0:T(8,128)(2,1)S(1)} %convert_element_type.126), channel_id=1, source_target_pairs={{0,6},{2,2},{4,4},{6,8},{8,14},{10,10},{12,12},{14,16},{16,22},{18... | collective-permute-start | bytes 399368 | tf_op jit(solution)/shard_map/ppermute | solution.py:346
  58.0 8.5 %collective-permute-start.16 = (f16[65,8,128]{2,1,0:T(8,128)(2,1)S(1)}, f16[65,8,128]{2,1,0:T(8,128)(2,1)S(1)}, u32[]{:S(2)}, u32[]{:S(2)}) collective-permute-start(f16[65,8,128]{2,1,0:T(8,128)(2,1)S(1)} %convert_element_type.124), channel_id=1, source_target_pairs={{0,2},{2,4},{4,6},{6,0},{8,10},{10,12},{12,14},{14,8},{16,18},{18,... | collective-permute-start | bytes 399368 | tf_op jit(solution)/shard_map/ppermute | solution.py:335
  58.1 11.7 %collective-permute-start.9 = (f16[65,8,128]{2,1,0:T(8,128)(2,1)S(1)}, f16[65,8,128]{2,1,0:T(8,128)(2,1)S(1)}, u32[]{:S(2)}, u32[]{:S(2)}) collective-permute-start(f16[65,8,128]{2,1,0:T(8,128)(2,1)S(1)} %convert_element_type.110), channel_id=1, source_target_pairs={{0,6},{2,2},{4,4},{6,8},{8,14},{10,10},{12,12},{14,16},{16,22},{18... | collective-permute-start | bytes 399368 | tf_op jit(solution)/shard_map/ppermute | solution.py:346
  66.4 5.9 %collective-permute-start.8 = (f16[65,8,128]{2,1,0:T(8,128)(2,1)S(1)}, f16[65,8,128]{2,1,0:T(8,128)(2,1)S(1)}, u32[]{:S(2)}, u32[]{:S(2)}) collective-permute-start(f16[65,8,128]{2,1,0:T(8,128)(2,1)S(1)} %convert_element_type.108), channel_id=1, source_target_pairs={{0,2},{2,4},{4,6},{6,0},{8,10},{10,12},{12,14},{14,8},{16,18},{18,... | collective-permute-start | bytes 399368 | tf_op jit(solution)/shard_map/ppermute | solution.py:335
  66.6 5.9 %collective-permute-start.19 = (f32[1,32,8,128]{3,2,1,0:T(8,128)S(1)}, f32[1,32,8,128]{3,2,1,0:T(8,128)S(1)}, u32[]{:S(2)}, u32[]{:S(2)}) collective-permute-start(f32[1,32,8,128]{3,2,1,0:T(8,128)S(1)} %get-tuple-element.92), channel_id=1, source_target_pairs={{1,0},{0,1},{3,2},{2,3},{5,4},{4,5},{7,6},{6,7},{9,8},{8,9},{11,10... | collective-permute-start | bytes 393224 | tf_op jit(solution)/shard_map/ppermute | solution.py:323
  72.4 1.4 %collective-permute-start.18 = (f32[1,32,8,128]{3,2,1,0:T(8,128)S(1)}, f32[1,32,8,128]{3,2,1,0:T(8,128)S(1)}, u32[]{:S(2)}, u32[]{:S(2)}) collective-permute-start(f32[1,32,8,128]{3,2,1,0:T(8,128)S(1)} %get-tuple-element.91), channel_id=1, source_target_pairs={{1,0},{0,1},{3,2},{2,3},{5,4},{4,5},{7,6},{6,7},{9,8},{8,9},{11,10... | collective-permute-start | bytes 393224 | tf_op jit(solution)/shard_map/ppermute | solution.py:323

commit v2 on v0

--- a/solution.py
+++ b/solution.py
@@ -6,7 +6,6 @@
 from jax.experimental import pallas as pl
 from jax.experimental.pallas import tpu as pltpu
 from jax.sharding import PartitionSpec as P
-
 
 HOPS = 4
 SUB = 8
@@ -78,24 +77,13 @@
 TOP = 13.0
 
 
-def take_in(cases, use):
-    def run(message, previous):
-        count = message.shape[0] - 1
-        back = jnp.exp2(message[count] - TOP)
-        pieces, columns, height, _ = previous.shape
-        for piece, j, at, b, m in tiles_of(pieces, columns, height):
-            use(piece, j, at, b, message[m] * back - previous[piece, j, at, :])
-
-    for chosen, message, previous in cases:
-        pl.when(chosen)(functools.partial(run, message, previous))
-
-
-def ends_of_ring():
-    here = lax.axis_index("seg")
-    return here == lax.axis_size("seg") - 1, here == 0
-
-
-def propagate_kernel(pieces, index, first, last, final, *refs):
+def scales(largest):
+    largest = jnp.broadcast_to(jnp.max(largest, axis=(0, 1), keepdims=True), (SUB, LANE))
+    power = jnp.clip(jnp.floor(jnp.log2(largest)), -100.0, 100.0)
+    return power, jnp.exp2(TOP - power), jnp.exp2(power - TOP)
+
+
+def propagate_kernel(pieces, index, first, final, *refs):
     refs = list(refs)
     take = lambda count: [refs.pop(0) for _ in range(count)]
     velocity = take(pieces)
@@ -104,53 +92,45 @@
     if first:
         previous = take(pieces)
     else:
-        previous, missed, message = take(3)
-        wrapped = None if last else take(1)[0]
-        (start,) = take(1)
+        previous, missed, message, start = take(4)
     (sent,) = take(1)
     error = None if final else take(1)[0]
     ping, pong = refs
-    at_last, at_first = ends_of_ring()
-
-    @pl.when(at_last if last else jnp.logical_not(at_last))
-    def _():
-        def use(piece, j, at, b, value):
+
+    most, carried = None, None
+    back = None if first else jnp.exp2(message[count] - TOP)
+    for piece, j, at, b, m in tiles_of(pieces, columns, height):
+        if first:
+            value = previous[piece][index, j, at, :]
+        else:
+            value = message[m] * back - previous[piece, j, at, :]
             start[piece, j, at, :] = value
-            place(ping, rows, j, b, value)
-
-        if first:
-            for piece, j, at, b, m in tiles_of(pieces, columns, height):
-                place(ping, rows, j, b, previous[piece][index, j, at, :])
-        elif last:
-            take_in([(at_last, message, previous)], use)
-        else:
-            take_in([(at_first, wrapped, previous), (jnp.logical_not(at_first), message, previous)], use)
-
-        done = advance(velocity, ping, pong, pieces)
-        largest = None
-        for piece, j, at, b, m in tiles_of(pieces, columns, height):
-            value = 0.2**depth * done[j, pl.ds(SUB + SUB * b, SUB), :]
-            if not first:
-                value = value + missed[m]
-            sent[m] = value
-            size = jnp.abs(value)
-            largest = size if largest is None else jnp.maximum(largest, size)
-        largest = jnp.broadcast_to(jnp.max(largest, axis=(0, 1), keepdims=True), (SUB, LANE))
-        power = jnp.clip(jnp.floor(jnp.log2(largest)), -100.0, 100.0)
-        scale, back = jnp.exp2(TOP - power), jnp.exp2(power - TOP)
-        sent[count] = power
-        for m in range(count):
-            value = sent[m]
-            scaled = value * scale
-            wide = scaled * 8193.0
-            short = wide - (wide - scaled)
-            sent[m] = short
-            if not final:
-                error[m] = short * back - value
-
-
-@functools.partial(jax.jit, static_argnames=("index", "last", "final"))
-def propagate(velocity, state, index=0, last=False, final=False):
+            size = jnp.abs(missed[m])
+            carried = size if carried is None else jnp.maximum(carried, size)
+        place(ping, rows, j, b, value)
+        size = jnp.abs(value)
+        most = size if most is None else jnp.maximum(most, size)
+    bound = 1.01 * 1.38**depth * jnp.max(most, axis=(0, 1), keepdims=True)
+    if not first:
+        bound = bound + jnp.max(carried, axis=(0, 1), keepdims=True)
+    power, scale, back = scales(jnp.broadcast_to(bound, (SUB, LANE)))
+    sent[count] = power
+
+    done = advance(velocity, ping, pong, pieces)
+    for piece, j, at, b, m in tiles_of(pieces, columns, height):
+        value = 0.2**depth * done[j, pl.ds(SUB + SUB * b, SUB), :]
+        if not first:
+            value = value + missed[m]
+        scaled = value * scale
+        wide = scaled * 8193.0
+        short = wide - (wide - scaled)
+        sent[m] = short
+        if not final:
+            error[m] = short * back - value
+
+
+@functools.partial(jax.jit, static_argnames=("index", "final"))
+def propagate(velocity, state, index=0, final=False):
     pieces = len(velocity)
     _, _, columns, height, lane = velocity[0].shape
     count = pieces * columns * height // SUB
@@ -161,37 +141,34 @@
     scratch = pltpu.VMEM((columns, pieces * height + 2 * SUB, lane), jnp.float32)
     args = [*velocity, *state]
     return pl.pallas_call(
-        functools.partial(propagate_kernel, pieces, index, first, last, final),
+        functools.partial(propagate_kernel, pieces, index, first, final),
         out_shape=outs,
         in_specs=[VMEM] * len(args),
         out_specs=[VMEM] * len(outs),
         scratch_shapes=[scratch, scratch],
         compiler_params=pltpu.CompilerParams(vmem_limit_bytes=16 << 20),
-        name="propagate_last" if last else "propagate",
+        name="propagate",
     )(*args)
 
 
-def residual_kernel(message, wrapped, previous, previous_last, *outs):
-    def use(piece, j, at, b, value):
-        outs[piece][0, j, at, :] = value
-
-    at_last, at_first = ends_of_ring()
-    rest = jnp.logical_not(jnp.logical_or(at_last, at_first))
-    cases = [(at_last, message, previous_last), (at_first, wrapped, previous), (rest, message, previous)]
-    take_in(cases, use)
+def residual_kernel(message, previous, *outs):
+    pieces, columns, height, _ = previous.shape
+    back = jnp.exp2(message[message.shape[0] - 1] - TOP)
+    for piece, j, at, b, m in tiles_of(pieces, columns, height):
+        outs[piece][0, j, at, :] = message[m] * back - previous[piece, j, at, :]
 
 
 @jax.jit
-def last_residual(*state):
-    pieces, columns, height, lane = state[2].shape
+def last_residual(message, previous):
+    pieces, columns, height, lane = previous.shape
     return pl.pallas_call(
         residual_kernel,
         out_shape=[jax.ShapeDtypeStruct((1, columns, height, lane), jnp.float32)] * pieces,
-        in_specs=[VMEM] * len(state),
+        in_specs=[VMEM, VMEM],
         out_specs=[VMEM] * pieces,
         compiler_params=pltpu.CompilerParams(vmem_limit_bytes=16 << 20),
         name="residual",
-    )(*state)
+    )(message, previous)
 
 
 def rows_kernel(pieces, index, *refs):
@@ -315,13 +292,13 @@
     return lax.ppermute(value, "slab", [((i + distance) % size, i) for i in range(size)])
 
 
-def to_next(value, segments=None):
+def to_next(value):
     size = lax.axis_size("seg")
-    return lax.ppermute(value, "seg", [(i, (i + 1) % size) for i in segments or range(size)])
-
-
-def sent_short(message, segments=None):
-    return to_next(message.astype(jnp.float16), segments).astype(jnp.float32)
+    return lax.ppermute(value, "seg", [(i, (i + 1) % size) for i in range(size)])
+
+
+def sent_short(message):
+    return to_next(message.astype(jnp.float16)).astype(jnp.float32)
 
 
 def split_vectors(vectors, velocity):
@@ -336,28 +313,19 @@
     for d in range(1, slabs):
         start.append(from_slab(part(slabs - d), d))
         speeds.append(from_slab(velocity, d))
-    end = lax.axis_size("seg") - 1
     previous = [jnp.concatenate([part[i : i + 1] for part in start], 0) for i in range(share)]
-    own, ends = list(previous), list(previous)
-    arrived, wrapped, missed, missed_end = [[None] * share for _ in range(4)]
+    arrived, missed = [None] * share, [None] * share
     for hop in range(HOPS):
         for i in range(share):
+            final = hop + 1 == HOPS
             if hop == 0:
-                state_end, state = start, start
+                out = list(propagate(speeds, start, i, final=final))
             else:
-                state_end = (ends[i], missed_end[i], arrived[i])
-                state = (own[i], missed[i], arrived[i], wrapped[i])
-            final, index = hop + 1 == HOPS, i if hop == 0 else 0
-            out_end = list(propagate(speeds, state_end, index, last=True, final=final))
-            out = list(propagate(speeds, state, index, final=final))
-            if hop:
-                ends[i], own[i] = out_end.pop(0), out.pop(0)
-            if not final:
-                missed_end[i], missed[i] = out_end.pop(), out.pop()
-            sent_end, sent = out_end[0], out[0]
-            wrapped[i] = sent_short(sent_end, [end])
-            arrived[i] = sent_short(sent, range(end))
-    parts = [last_residual(arrived[i], wrapped[i], own[i], ends[i]) for i in range(share)]
+                out = list(propagate(speeds, (previous[i], missed[i], arrived[i]), final=final))
+                previous[i] = out.pop(0)
+            missed[i] = None if final else out[1]
+            arrived[i] = sent_short(out[0])
+    parts = [last_residual(arrived[i], previous[i]) for i in range(share)]
     residual = []
     for d in range(slabs):
         for i in range(share):
@@ -376,7 +344,7 @@
 
     speeds = pieces(velocity)
     begun = vectors
-    for _ in range(HOPS):
+    for hop in range(HOPS):
         state = pieces(begun)
         arrived = [to_next(propagate_rows(speeds, state, i)) for i in range(vectors.shape[0])]
         begun = jnp.concatenate(arrived, 0) - begun
@@ -387,9 +355,8 @@
     vectors, velocity = tiled(block[0]), tiled(base_velocity[0])
     even = vectors.shape[0] % lax.axis_size("slab") == 0
     share, residual = (split_vectors if even else split_rows)(vectors, velocity)
-    axes = ("seg", "slab")
     gram = local_gram(share, residual, lax.axis_size("seg") * lax.axis_size("slab"))
-    gram = lax.all_to_all(gram, axes, 0, 0, tiled=True)
+    gram = lax.all_to_all(gram, ("seg", "slab"), 0, 0, tiled=True)
     return untiled(solved(share, gram, residual))[None]
 
 

time: 76.9 us -> 62.9 us (0.82)
  starting transfers between devices: 27.9 us -> 5.6 us
  waiting for transfers between devices: 18.4 us -> 31.7 us
  blocking collectives: 12.8 us -> 8.96 us
    ppermute x16 -> x8, starting transfers between devices: 27.1 us -> 4.79 us  [to_next(): lax.ppermute(value, 'seg', [(i, (i + 1) % size) for i in range(size)])]
    ppermute x16 -> x8, waiting for transfers between devices: 15.5 us -> 28.8 us  [to_next(): lax.ppermute(value, 'seg', [(i, (i + 1) % size) for i in range(size)])]
    all_to_all x1, blocking collectives: 12.8 us -> 8.96 us  [shards(): gram = lax.all_to_all(gram, ('seg', 'slab'), 0, 0, tiled=True)]
    pallas_call x16 -> x8, Pallas kernels: 13.5 us -> 13.3 us  [propagate(): pl.pallas_call(functools.partial(propagate_kernel, pieces, index, first,...]
  transfers between devices with their start and end apart: 20 -> 12, of which waited for: 8 -> 9; matrix products, arithmetic and copies ran while one was open for 2% -> 2% of each run, Pallas kernels for 18% -> 19%
where the time goes in v2:
time: 62.9 us; the launch traced here: 62.7 us
  waiting for transfers between devices  31.7 us (50%)
  Pallas kernels  14.7 us (23%)
  blocking collectives  8.96 us (14%)
  starting transfers between devices  5.6 us (9%)
  local copies, waits for them, and re-layouts  1.1 us (2%)
    ppermute x8, waiting for transfers between devices, to_next(): lax.ppermute(value, 'seg', [(i, (i + 1) % size) for i in range(size)])  28.8 us
    pallas_call x8, Pallas kernels, propagate(): pl.pallas_call(functools.partial(propagate_kernel, pieces, index, first,...  13.3 us
    all_to_all x1, blocking collectives, shards(): gram = lax.all_to_all(gram, ('seg', 'slab'), 0, 0, tiled=True)  8.96 us
    ppermute x8, starting transfers between devices, to_next(): lax.ppermute(value, 'seg', [(i, (i + 1) % size) for i in range(size)])  4.79 us
    ppermute x4, waiting for transfers between devices, from_slab(): lax.ppermute(value, 'slab', [((i + distance) % size, i) for i in range(si...  2.95 us
  transfers between devices with their start and end apart: 12, of which 9 were waited for; matrix products, arithmetic and copies ran while one was open for 2% of the time, Pallas kernels for 19%

profile of v2, /device:TPU:0, one launch (start us, length us, event | category | flops | bytes accessed | tf_op | source)
XLA Modules:
  0.0 62.7 jit_solution(14789083295320304740)
XLA Ops:
  0.0 0.5 collective-permute-start
  0.5 1.1 %dynamic-slice_bitcast_fusion.1 = (f32[2,32,8,128]{3,2,1,0:T(8,128)S(1)}, f32[2,32,8,128]{3,2,1,0:T(8,128)S(1)}) fusion(f32[4,8,32,128]{3,1,2,0:T(8,128)} %bitcast.26, s32[]{:T(128)S(6)} %select_n.6, s32[]{:T(128)S(6)} %select_n.7), kind=kLoop, calls=%fused_computation.3 | loop fusion | bytes 1048584 | tf_op jit(solution)/shard_map/dynamic_slice | solution.py:310
  1.8 1.6 %collective-permute-done.1.refs_3_ = f32[2,32,8,128]{3,2,1,0:T(8,128)S(1)} collective-permute-done((f32[2,32,8,128]{3,2,1,0:T(8,128)S(1)}, f32[2,32,8,128]{3,2,1,0:T(8,128)S(1)}, u32[]{:S(2)}, u32[]{:S(2)}) %collective-permute-start.1) | collective-permute-done | bytes 262176 | tf_op jit(solution)/shard_map/ppermute | solution.py:292
  3.4 1.6 %propagate.12 = (f32[65,8,128]{2,1,0:T(8,128)S(1)}, f32[64,8,128]{2,1,0:T(8,128)S(1)}) custom-call(bf16[8,2,32,8,128]{4,3,2,1,0:T(8,128)(2,1)S(1)} %bitcast.16, bf16[8,2,32,8,128]{4,3,2,1,0:T(8,128)(2,1)S(1)} %collective-permute-done.refs_1_, f32[2,32,8,128]{3,2,1,0:T(8,128)S(1)} %get-tuple-element.53.refs_2_, ...), custom_call_target="tpu_custom_call" | custom-call | tf_op jit(solution)/shard_map/jit(propagate)/propagate/pallas_call | solution.py:143
  5.0 2.9 %collective-permute-start.6 = (f16[65,8,128]{2,1,0:T(8,128)(2,1)S(1)}, f16[65,8,128]{2,1,0:T(8,128)(2,1)S(1)}, u32[]{:S(2)}, u32[]{:S(2)}) collective-permute-start(f16[65,8,128]{2,1,0:T(8,128)(2,1)S(1)} %convert_element_type.56), channel_id=1, source_target_pairs={{0,2},{2,4},{4,6},{6,8},{8,10},{10,12},{12,14},{14,16},{16,18},{18... | collective-permute-start | bytes 399368 | tf_op jit(solution)/shard_map/ppermute | solution.py:297
  8.0 1.6 %propagate.8 = (f32[65,8,128]{2,1,0:T(8,128)S(1)}, f32[64,8,128]{2,1,0:T(8,128)S(1)}) custom-call(bf16[8,2,32,8,128]{4,3,2,1,0:T(8,128)(2,1)S(1)} %bitcast.17, bf16[8,2,32,8,128]{4,3,2,1,0:T(8,128)(2,1)S(1)} %collective-permute-done.refs_1_, f32[2,32,8,128]{3,2,1,0:T(8,128)S(1)} %get-tuple-element.53.refs_2_, ...), custom_call_target="tpu_custom_call" | custom-call | tf_op jit(solution)/shard_map/jit(propagate)/propagate/pallas_call | solution.py:143
  9.6 1.5 %collective-permute-start.2 = (f16[65,8,128]{2,1,0:T(8,128)(2,1)S(1)}, f16[65,8,128]{2,1,0:T(8,128)(2,1)S(1)}, u32[]{:S(2)}, u32[]{:S(2)}) collective-permute-start(f16[65,8,128]{2,1,0:T(8,128)(2,1)S(1)} %convert_element_type.48), channel_id=1, source_target_pairs={{0,2},{2,4},{4,6},{6,8},{8,10},{10,12},{12,14},{14,16},{16,18},{18... | collective-permute-start | bytes 399368 | tf_op jit(solution)/shard_map/ppermute | solution.py:297
  11.2 4.6 %collective-permute-done.6 = f16[65,8,128]{2,1,0:T(8,128)(2,1)S(1)} collective-permute-done((f16[65,8,128]{2,1,0:T(8,128)(2,1)S(1)}, f16[65,8,128]{2,1,0:T(8,128)(2,1)S(1)}, u32[]{:S(2)}, u32[]{:S(2)}) %collective-permute-start.6) | collective-permute-done | bytes 133152 | tf_op jit(solution)/shard_map/ppermute | solution.py:297
  15.8 1.7 %propagate.13 = (f32[2,32,8,128]{3,2,1,0:T(8,128)S(1)}, f32[65,8,128]{2,1,0:T(8,128)S(1)}, f32[64,8,128]{2,1,0:T(8,128)S(1)}) custom-call(bf16[8,2,32,8,128]{4,3,2,1,0:T(8,128)(2,1)S(1)} %bitcast.18, bf16[8,2,32,8,128]{4,3,2,1,0:T(8,128)(2,1)S(1)} %collective-permute-done.refs_1_, f32[2,32,8,128]{3,2,1,0:T(8,128)S(1)} %pad_maximum_fusion.1.refs_2_, ...), custom_call_target="tpu_custom_call" | custom-call | tf_op jit(solution)/shard_map/jit(propagate)/propagate/pallas_call | solution.py:143
  17.7 1.0 %collective-permute-done.2 = f16[65,8,128]{2,1,0:T(8,128)(2,1)S(1)} collective-permute-done((f16[65,8,128]{2,1,0:T(8,128)(2,1)S(1)}, f16[65,8,128]{2,1,0:T(8,128)(2,1)S(1)}, u32[]{:S(2)}, u32[]{:S(2)}) %collective-permute-start.2) | collective-permute-done | bytes 133152 | tf_op jit(solution)/shard_map/ppermute | solution.py:297
  18.6 1.7 %propagate.9 = (f32[2,32,8,128]{3,2,1,0:T(8,128)S(1)}, f32[65,8,128]{2,1,0:T(8,128)S(1)}, f32[64,8,128]{2,1,0:T(8,128)S(1)}) custom-call(bf16[8,2,32,8,128]{4,3,2,1,0:T(8,128)(2,1)S(1)} %bitcast.19, bf16[8,2,32,8,128]{4,3,2,1,0:T(8,128)(2,1)S(1)} %collective-permute-done.refs_1_, f32[2,32,8,128]{3,2,1,0:T(8,128)S(1)} %pad_maximum_fusion.refs_2_, ...), custom_call_target="tpu_custom_call" | custom-call | tf_op jit(solution)/shard_map/jit(propagate)/propagate/pallas_call | solution.py:143
  20.4 6.3 %collective-permute-done.7 = f16[65,8,128]{2,1,0:T(8,128)(2,1)S(1)} collective-permute-done((f16[65,8,128]{2,1,0:T(8,128)(2,1)S(1)}, f16[65,8,128]{2,1,0:T(8,128)(2,1)S(1)}, u32[]{:S(2)}, u32[]{:S(2)}) %collective-permute-start.7) | collective-permute-done | bytes 133152 | tf_op jit(solution)/shard_map/ppermute | solution.py:297
  26.8 1.7 %propagate.14 = (f32[2,32,8,128]{3,2,1,0:T(8,128)S(1)}, f32[65,8,128]{2,1,0:T(8,128)S(1)}, f32[64,8,128]{2,1,0:T(8,128)S(1)}) custom-call(bf16[8,2,32,8,128]{4,3,2,1,0:T(8,128)(2,1)S(1)} %bitcast.20, bf16[8,2,32,8,128]{4,3,2,1,0:T(8,128)(2,1)S(1)} %collective-permute-done.refs_1_, f32[2,32,8,128]{3,2,1,0:T(8,128)S(1)} %get-tuple-element.42.refs_2_, ...), custom_call_target="tpu_custom_call" | custom-call | tf_op jit(solution)/shard_map/jit(propagate)/propagate/pallas_call | solution.py:143
  28.5 0.5 collective-permute-done.3
  29.1 1.7 %propagate.10 = (f32[2,32,8,128]{3,2,1,0:T(8,128)S(1)}, f32[65,8,128]{2,1,0:T(8,128)S(1)}, f32[64,8,128]{2,1,0:T(8,128)S(1)}) custom-call(bf16[8,2,32,8,128]{4,3,2,1,0:T(8,128)(2,1)S(1)} %bitcast.21, bf16[8,2,32,8,128]{4,3,2,1,0:T(8,128)(2,1)S(1)} %collective-permute-done.refs_1_, f32[2,32,8,128]{3,2,1,0:T(8,128)S(1)} %get-tuple-element.31.refs_2_, ...), custom_call_target="tpu_custom_call" | custom-call | tf_op jit(solution)/shard_map/jit(propagate)/propagate/pallas_call | solution.py:143
  30.9 7.6 %collective-permute-done.8 = f16[65,8,128]{2,1,0:T(8,128)(2,1)S(1)} collective-permute-done((f16[65,8,128]{2,1,0:T(8,128)(2,1)S(1)}, f16[65,8,128]{2,1,0:T(8,128)(2,1)S(1)}, u32[]{:S(2)}, u32[]{:S(2)}) %collective-permute-start.8) | collective-permute-done | bytes 133152 | tf_op jit(solution)/shard_map/ppermute | solution.py:297
  38.5 1.7 %propagate.15 = (f32[2,32,8,128]{3,2,1,0:T(8,128)S(1)}, f32[65,8,128]{2,1,0:T(8,128)S(1)}) custom-call(bf16[8,2,32,8,128]{4,3,2,1,0:T(8,128)(2,1)S(1)} %bitcast.22, bf16[8,2,32,8,128]{4,3,2,1,0:T(8,128)(2,1)S(1)} %collective-permute-done.refs_1_, f32[2,32,8,128]{3,2,1,0:T(8,128)S(1)} %get-tuple-element.45.refs_2_, ...), custom_call_target="tpu_custom_call" | custom-call | tf_op jit(solution)/shard_map/jit(propagate)/propagate/pallas_call | solution.py:143
  40.3 1.7 %propagate.11 = (f32[2,32,8,128]{3,2,1,0:T(8,128)S(1)}, f32[65,8,128]{2,1,0:T(8,128)S(1)}) custom-call(bf16[8,2,32,8,128]{4,3,2,1,0:T(8,128)(2,1)S(1)} %bitcast.23, bf16[8,2,32,8,128]{4,3,2,1,0:T(8,128)(2,1)S(1)} %collective-permute-done.refs_1_, f32[2,32,8,128]{3,2,1,0:T(8,128)S(1)} %get-tuple-element.34.refs_2_, ...), custom_call_target="tpu_custom_call" | custom-call | tf_op jit(solution)/shard_map/jit(propagate)/propagate/pallas_call | solution.py:143
  42.0 7.5 %collective-permute-done.9 = f16[65,8,128]{2,1,0:T(8,128)(2,1)S(1)} collective-permute-done((f16[65,8,128]{2,1,0:T(8,128)(2,1)S(1)}, f16[65,8,128]{2,1,0:T(8,128)(2,1)S(1)}, u32[]{:S(2)}, u32[]{:S(2)}) %collective-permute-start.9) | collective-permute-done | bytes 133152 | tf_op jit(solution)/shard_map/ppermute | solution.py:297
  49.7 1.3 %collective-permute-done.5 = f16[65,8,128]{2,1,0:T(8,128)(2,1)S(1)} collective-permute-done((f16[65,8,128]{2,1,0:T(8,128)(2,1)S(1)}, f16[65,8,128]{2,1,0:T(8,128)(2,1)S(1)}, u32[]{:S(2)}, u32[]{:S(2)}) %collective-permute-start.5) | collective-permute-done | bytes 133152 | tf_op jit(solution)/shard_map/ppermute | solution.py:297
  51.2 1.3 %collective-permute-done.10.refs_2_ = f32[1,32,8,128]{3,2,1,0:T(8,128)S(1)} collective-permute-done((f32[1,32,8,128]{3,2,1,0:T(8,128)S(1)}, f32[1,32,8,128]{3,2,1,0:T(8,128)S(1)}, u32[]{:S(2)}, u32[]{:S(2)}) %collective-permute-start.10) | collective-permute-done | bytes 131104 | tf_op jit(solution)/shard_map/ppermute | solution.py:292
  52.5 0.2 gram.1
  52.7 9.0 %all_to_all.11 = f32[32,1,128]{2,1,0:T(1,128)S(1)} all-to-all(f32[32,1,128]{2,1,0:T(1,128)S(1)} %bitcast.25), channel_id=1, replica_groups=mesh['seg'=16,'slab'=2] {'seg','slab'}, dimensions={0} | all-to-all | bytes 32768 | tf_op jit(solution)/shard_map/all_to_all | solution.py:359
  61.6 1.1 %solve.1 = f32[4,32,8,128]{3,2,1,0:T(8,128)} custom-call(f32[32,128]{1,0:T(8,128)S(1)} %bitcast.24, f32[1,32,8,128]{3,2,1,0:T(8,128)S(1)} %get-tuple-element.39.refs_0_, f32[1,32,8,128]{3,2,1,0:T(8,128)S(1)} %get-tuple-element.50.refs_1_, f32[1,32,8,128]{3,2,1,0:T(8,128)S(1)} %collective-permute-done.10.refs_2_, ...), custom_call_target="tpu_custom_call" | custom-call | tf_op jit(solution)/shard_map/solve/pallas_call | solution.py:280
  (36 shorter events, 1.2 us)
Async XLA Ops:
  0.0 3.4 %copy-start = (bf16[1,8,2,8,4096]{4,3,2,1,0:T(8,128)(2,1)S(1)}, bf16[1,8,2,8,4096]{4,3,2,1,0:T(8,128)(2,1)}, u32[]{:S(2)}) copy-start(bf16[1,8,2,8,4096]{4,3,2,1,0:T(8,128)(2,1)} %param.3) | copy-start | bytes 3145732
  0.0 3.4 %collective-permute-start = (bf16[8,2,32,8,128]{4,3,2,1,0:T(8,128)(2,1)}, bf16[8,2,32,8,128]{4,3,2,1,0:T(8,128)(2,1)S(1)}, u32[]{:S(2)}, u32[]{:S(2)}) collective-permute-start(bf16[8,2,32,8,128]{4,3,2,1,0:T(8,128)(2,1)} %bitcast.15), channel_id=1, source_target_pairs={{1,0},{0,1},{3,2},{2,3},{5,4},{4,5},{7,6},{6,7},{9,8},{8,9},{11,10... | collective-permute-start | bytes 3145736 | tf_op jit(solution)/shard_map/ppermute | solution.py:292
  1.6 1.8 %collective-permute-start.1 = (f32[2,32,8,128]{3,2,1,0:T(8,128)S(1)}, f32[2,32,8,128]{3,2,1,0:T(8,128)S(1)}, u32[]{:S(2)}, u32[]{:S(2)}) collective-permute-start(f32[2,32,8,128]{3,2,1,0:T(8,128)S(1)} %get-tuple-element.54), channel_id=1, source_target_pairs={{1,0},{0,1},{3,2},{2,3},{5,4},{4,5},{7,6},{6,7},{9,8},{8,9},{11,10... | collective-permute-start | bytes 786440 | tf_op jit(solution)/shard_map/ppermute | solution.py:292
  5.0 10.8 %collective-permute-start.6 = (f16[65,8,128]{2,1,0:T(8,128)(2,1)S(1)}, f16[65,8,128]{2,1,0:T(8,128)(2,1)S(1)}, u32[]{:S(2)}, u32[]{:S(2)}) collective-permute-start(f16[65,8,128]{2,1,0:T(8,128)(2,1)S(1)} %convert_element_type.56), channel_id=1, source_target_pairs={{0,2},{2,4},{4,6},{6,8},{8,10},{10,12},{12,14},{14,16},{16,18},{18... | collective-permute-start | bytes 399368 | tf_op jit(solution)/shard_map/ppermute | solution.py:297
  9.6 9.0 %collective-permute-start.2 = (f16[65,8,128]{2,1,0:T(8,128)(2,1)S(1)}, f16[65,8,128]{2,1,0:T(8,128)(2,1)S(1)}, u32[]{:S(2)}, u32[]{:S(2)}) collective-permute-start(f16[65,8,128]{2,1,0:T(8,128)(2,1)S(1)} %convert_element_type.48), channel_id=1, source_target_pairs={{0,2},{2,4},{4,6},{6,8},{8,10},{10,12},{12,14},{14,16},{16,18},{18... | collective-permute-start | bytes 399368 | tf_op jit(solution)/shard_map/ppermute | solution.py:297
  17.6 9.2 %collective-permute-start.7 = (f16[65,8,128]{2,1,0:T(8,128)(2,1)S(1)}, f16[65,8,128]{2,1,0:T(8,128)(2,1)S(1)}, u32[]{:S(2)}, u32[]{:S(2)}) collective-permute-start(f16[65,8,128]{2,1,0:T(8,128)(2,1)S(1)} %convert_element_type.58), channel_id=1, source_target_pairs={{0,2},{2,4},{4,6},{6,8},{8,10},{10,12},{12,14},{14,16},{16,18},{18... | collective-permute-start | bytes 399368 | tf_op jit(solution)/shard_map/ppermute | solution.py:297
  20.4 8.7 %collective-permute-start.3 = (f16[65,8,128]{2,1,0:T(8,128)(2,1)S(1)}, f16[65,8,128]{2,1,0:T(8,128)(2,1)S(1)}, u32[]{:S(2)}, u32[]{:S(2)}) collective-permute-start(f16[65,8,128]{2,1,0:T(8,128)(2,1)S(1)} %convert_element_type.50), channel_id=1, source_target_pairs={{0,2},{2,4},{4,6},{6,8},{8,10},{10,12},{12,14},{14,16},{16,18},{18... | collective-permute-start | bytes 399368 | tf_op jit(solution)/shard_map/ppermute | solution.py:297
  28.5 10.0 %collective-permute-start.8 = (f16[65,8,128]{2,1,0:T(8,128)(2,1)S(1)}, f16[65,8,128]{2,1,0:T(8,128)(2,1)S(1)}, u32[]{:S(2)}, u32[]{:S(2)}) collective-permute-start(f16[65,8,128]{2,1,0:T(8,128)(2,1)S(1)} %convert_element_type.60), channel_id=1, source_target_pairs={{0,2},{2,4},{4,6},{6,8},{8,10},{10,12},{12,14},{14,16},{16,18},{18... | collective-permute-start | bytes 399368 | tf_op jit(solution)/shard_map/ppermute | solution.py:297
  30.8 9.4 %collective-permute-start.4 = (f16[65,8,128]{2,1,0:T(8,128)(2,1)S(1)}, f16[65,8,128]{2,1,0:T(8,128)(2,1)S(1)}, u32[]{:S(2)}, u32[]{:S(2)}) collective-permute-start(f16[65,8,128]{2,1,0:T(8,128)(2,1)S(1)} %convert_element_type.52), channel_id=1, source_target_pairs={{0,2},{2,4},{4,6},{6,8},{8,10},{10,12},{12,14},{14,16},{16,18},{18... | collective-permute-start | bytes 399368 | tf_op jit(solution)/shard_map/ppermute | solution.py:297
  40.2 9.4 %collective-permute-start.9 = (f16[65,8,128]{2,1,0:T(8,128)(2,1)S(1)}, f16[65,8,128]{2,1,0:T(8,128)(2,1)S(1)}, u32[]{:S(2)}, u32[]{:S(2)}) collective-permute-start(f16[65,8,128]{2,1,0:T(8,128)(2,1)S(1)} %convert_element_type.62), channel_id=1, source_target_pairs={{0,2},{2,4},{4,6},{6,8},{8,10},{10,12},{12,14},{14,16},{16,18},{18... | collective-permute-start | bytes 399368 | tf_op jit(solution)/shard_map/ppermute | solution.py:297
  42.0 9.0 %collective-permute-start.5 = (f16[65,8,128]{2,1,0:T(8,128)(2,1)S(1)}, f16[65,8,128]{2,1,0:T(8,128)(2,1)S(1)}, u32[]{:S(2)}, u32[]{:S(2)}) collective-permute-start(f16[65,8,128]{2,1,0:T(8,128)(2,1)S(1)} %convert_element_type.54), channel_id=1, source_target_pairs={{0,2},{2,4},{4,6},{6,8},{8,10},{10,12},{12,14},{14,16},{16,18},{18... | collective-permute-start | bytes 399368 | tf_op jit(solution)/shard_map/ppermute | solution.py:297
  49.6 1.5 %collective-permute-start.11 = (f32[1,32,8,128]{3,2,1,0:T(8,128)S(1)}, f32[1,32,8,128]{3,2,1,0:T(8,128)S(1)}, u32[]{:S(2)}, u32[]{:S(2)}) collective-permute-start(f32[1,32,8,128]{3,2,1,0:T(8,128)S(1)} %get-tuple-element.52), channel_id=1, source_target_pairs={{1,0},{0,1},{3,2},{2,3},{5,4},{4,5},{7,6},{6,7},{9,8},{8,9},{11,10... | collective-permute-start | bytes 393224 | tf_op jit(solution)/shard_map/ppermute | solution.py:292
  51.1 1.4 %collective-permute-start.10 = (f32[1,32,8,128]{3,2,1,0:T(8,128)S(1)}, f32[1,32,8,128]{3,2,1,0:T(8,128)S(1)}, u32[]{:S(2)}, u32[]{:S(2)}) collective-permute-start(f32[1,32,8,128]{3,2,1,0:T(8,128)S(1)} %get-tuple-element.51), channel_id=1, source_target_pairs={{1,0},{0,1},{3,2},{2,3},{5,4},{4,5},{7,6},{6,7},{9,8},{8,9},{11,10... | collective-permute-start | bytes 393224 | tf_op jit(solution)/shard_map/ppermute | solution.py:292

commit v3 on v2

--- a/solution.py
+++ b/solution.py
@@ -24,7 +24,7 @@
     return jnp.swapaxes(tiles, -3, -2).reshape(lead + (height, count * lane))
 
 
-def advance(velocity, ping, pong, pieces):
+def advance(velocity, ping, pong, pieces, unroll=False):
     depth, _, columns, height, _ = velocity[0].shape
     rows = pieces * height
     lane = lax.broadcasted_iota(jnp.int32, (SUB, LANE), 1)
@@ -52,7 +52,11 @@
         step(2 * i + 1, pong, ping)
         return carry
 
-    lax.fori_loop(0, depth // 2, pair, 0)
+    if unroll:
+        for i in range(depth // 2):
+            pair(i, 0)
+    else:
+        lax.fori_loop(0, depth // 2, pair, 0)
     if depth % 2:
         step(depth - 1, ping, pong)
         return pong
@@ -116,7 +120,7 @@
     power, scale, back = scales(jnp.broadcast_to(bound, (SUB, LANE)))
     sent[count] = power
 
-    done = advance(velocity, ping, pong, pieces)
+    done = advance(velocity, ping, pong, pieces, True)
     for piece, j, at, b, m in tiles_of(pieces, columns, height):
         value = 0.2**depth * done[j, pl.ds(SUB + SUB * b, SUB), :]
         if not first:

time: 62.9 us -> 62.3 us (level)
  Pallas kernels: 14.7 us -> 13.2 us
  waiting for transfers between devices: 31.7 us -> 32.6 us
    pallas_call x8, Pallas kernels: 13.3 us -> 11.8 us  [propagate(): pl.pallas_call(functools.partial(propagate_kernel, pieces, index, first,...]
    ppermute x8, waiting for transfers between devices: 28.8 us -> 29.7 us  [to_next(): lax.ppermute(value, 'seg', [(i, (i + 1) % size) for i in range(size)])]
  transfers between devices with their start and end apart: 12 -> 12, of which waited for: 9 -> 9; matrix products, arithmetic and copies ran while one was open for 2% -> 2% of each run, Pallas kernels for 19% -> 17%
where the time goes in v3:
time: 62.3 us; the launch traced here: 62.2 us
  waiting for transfers between devices  32.6 us (52%)
  Pallas kernels  13.2 us (21%)
  blocking collectives  8.86 us (14%)
  starting transfers between devices  5.78 us (9%)
  local copies, waits for them, and re-layouts  1.1 us (2%)
    ppermute x8, waiting for transfers between devices, to_next(): lax.ppermute(value, 'seg', [(i, (i + 1) % size) for i in range(size)])  29.7 us
    pallas_call x8, Pallas kernels, propagate(): pl.pallas_call(functools.partial(propagate_kernel, pieces, index, first,...  11.8 us
    all_to_all x1, blocking collectives, shards(): gram = lax.all_to_all(gram, ('seg', 'slab'), 0, 0, tiled=True)  8.86 us
    ppermute x8, starting transfers between devices, to_next(): lax.ppermute(value, 'seg', [(i, (i + 1) % size) for i in range(size)])  4.98 us
    ppermute x4, waiting for transfers between devices, from_slab(): lax.ppermute(value, 'slab', [((i + distance) % size, i) for i in range(si...  2.95 us
  transfers between devices with their start and end apart: 12, of which 9 were waited for; matrix products, arithmetic and copies ran while one was open for 2% of the time, Pallas kernels for 17%

profile of v3, /device:TPU:0, one launch (start us, length us, event | category | flops | bytes accessed | tf_op | source)
XLA Modules:
  0.0 62.2 jit_solution(3235068996338507)
XLA Ops:
  0.0 0.5 collective-permute-start
  0.5 1.1 %dynamic-slice_bitcast_fusion.1 = (f32[2,32,8,128]{3,2,1,0:T(8,128)S(1)}, f32[2,32,8,128]{3,2,1,0:T(8,128)S(1)}) fusion(f32[4,8,32,128]{3,1,2,0:T(8,128)} %bitcast.26, s32[]{:T(128)S(6)} %select_n.6, s32[]{:T(128)S(6)} %select_n.7), kind=kLoop, calls=%fused_computation.3 | loop fusion | bytes 1048584 | tf_op jit(solution)/shard_map/dynamic_slice | solution.py:314
  1.8 1.6 %collective-permute-done.1.refs_3_ = f32[2,32,8,128]{3,2,1,0:T(8,128)S(1)} collective-permute-done((f32[2,32,8,128]{3,2,1,0:T(8,128)S(1)}, f32[2,32,8,128]{3,2,1,0:T(8,128)S(1)}, u32[]{:S(2)}, u32[]{:S(2)}) %collective-permute-start.1) | collective-permute-done | bytes 262176 | tf_op jit(solution)/shard_map/ppermute | solution.py:296
  3.4 1.5 %propagate.12 = (f32[65,8,128]{2,1,0:T(8,128)S(1)}, f32[64,8,128]{2,1,0:T(8,128)S(1)}) custom-call(bf16[8,2,32,8,128]{4,3,2,1,0:T(8,128)(2,1)S(1)} %bitcast.16, bf16[8,2,32,8,128]{4,3,2,1,0:T(8,128)(2,1)S(1)} %collective-permute-done.refs_1_, f32[2,32,8,128]{3,2,1,0:T(8,128)S(1)} %get-tuple-element.53.refs_2_, ...), custom_call_target="tpu_custom_call" | custom-call | tf_op jit(solution)/shard_map/jit(propagate)/propagate/pallas_call | solution.py:147
  4.9 2.9 %collective-permute-start.6 = (f16[65,8,128]{2,1,0:T(8,128)(2,1)S(1)}, f16[65,8,128]{2,1,0:T(8,128)(2,1)S(1)}, u32[]{:S(2)}, u32[]{:S(2)}) collective-permute-start(f16[65,8,128]{2,1,0:T(8,128)(2,1)S(1)} %convert_element_type.56), channel_id=1, source_target_pairs={{0,2},{2,4},{4,6},{6,8},{8,10},{10,12},{12,14},{14,16},{16,18},{18... | collective-permute-start | bytes 399368 | tf_op jit(solution)/shard_map/ppermute | solution.py:301
  7.8 1.5 %propagate.8 = (f32[65,8,128]{2,1,0:T(8,128)S(1)}, f32[64,8,128]{2,1,0:T(8,128)S(1)}) custom-call(bf16[8,2,32,8,128]{4,3,2,1,0:T(8,128)(2,1)S(1)} %bitcast.17, bf16[8,2,32,8,128]{4,3,2,1,0:T(8,128)(2,1)S(1)} %collective-permute-done.refs_1_, f32[2,32,8,128]{3,2,1,0:T(8,128)S(1)} %get-tuple-element.53.refs_2_, ...), custom_call_target="tpu_custom_call" | custom-call | tf_op jit(solution)/shard_map/jit(propagate)/propagate/pallas_call | solution.py:147
  9.3 1.5 %collective-permute-start.2 = (f16[65,8,128]{2,1,0:T(8,128)(2,1)S(1)}, f16[65,8,128]{2,1,0:T(8,128)(2,1)S(1)}, u32[]{:S(2)}, u32[]{:S(2)}) collective-permute-start(f16[65,8,128]{2,1,0:T(8,128)(2,1)S(1)} %convert_element_type.48), channel_id=1, source_target_pairs={{0,2},{2,4},{4,6},{6,8},{8,10},{10,12},{12,14},{14,16},{16,18},{18... | collective-permute-start | bytes 399368 | tf_op jit(solution)/shard_map/ppermute | solution.py:301
  10.9 5.0 %collective-permute-done.6 = f16[65,8,128]{2,1,0:T(8,128)(2,1)S(1)} collective-permute-done((f16[65,8,128]{2,1,0:T(8,128)(2,1)S(1)}, f16[65,8,128]{2,1,0:T(8,128)(2,1)S(1)}, u32[]{:S(2)}, u32[]{:S(2)}) %collective-permute-start.6) | collective-permute-done | bytes 133152 | tf_op jit(solution)/shard_map/ppermute | solution.py:301
  15.8 1.5 %propagate.13 = (f32[2,32,8,128]{3,2,1,0:T(8,128)S(1)}, f32[65,8,128]{2,1,0:T(8,128)S(1)}, f32[64,8,128]{2,1,0:T(8,128)S(1)}) custom-call(bf16[8,2,32,8,128]{4,3,2,1,0:T(8,128)(2,1)S(1)} %bitcast.18, bf16[8,2,32,8,128]{4,3,2,1,0:T(8,128)(2,1)S(1)} %collective-permute-done.refs_1_, f32[2,32,8,128]{3,2,1,0:T(8,128)S(1)} %pad_maximum_fusion.1.refs_2_, ...), custom_call_target="tpu_custom_call" | custom-call | tf_op jit(solution)/shard_map/jit(propagate)/propagate/pallas_call | solution.py:147
  17.5 1.0 %collective-permute-done.2 = f16[65,8,128]{2,1,0:T(8,128)(2,1)S(1)} collective-permute-done((f16[65,8,128]{2,1,0:T(8,128)(2,1)S(1)}, f16[65,8,128]{2,1,0:T(8,128)(2,1)S(1)}, u32[]{:S(2)}, u32[]{:S(2)}) %collective-permute-start.2) | collective-permute-done | bytes 133152 | tf_op jit(solution)/shard_map/ppermute | solution.py:301
  18.5 1.5 %propagate.9 = (f32[2,32,8,128]{3,2,1,0:T(8,128)S(1)}, f32[65,8,128]{2,1,0:T(8,128)S(1)}, f32[64,8,128]{2,1,0:T(8,128)S(1)}) custom-call(bf16[8,2,32,8,128]{4,3,2,1,0:T(8,128)(2,1)S(1)} %bitcast.19, bf16[8,2,32,8,128]{4,3,2,1,0:T(8,128)(2,1)S(1)} %collective-permute-done.refs_1_, f32[2,32,8,128]{3,2,1,0:T(8,128)S(1)} %pad_maximum_fusion.refs_2_, ...), custom_call_target="tpu_custom_call" | custom-call | tf_op jit(solution)/shard_map/jit(propagate)/propagate/pallas_call | solution.py:147
  20.1 6.5 %collective-permute-done.7 = f16[65,8,128]{2,1,0:T(8,128)(2,1)S(1)} collective-permute-done((f16[65,8,128]{2,1,0:T(8,128)(2,1)S(1)}, f16[65,8,128]{2,1,0:T(8,128)(2,1)S(1)}, u32[]{:S(2)}, u32[]{:S(2)}) %collective-permute-start.7) | collective-permute-done | bytes 133152 | tf_op jit(solution)/shard_map/ppermute | solution.py:301
  26.6 1.5 %propagate.14 = (f32[2,32,8,128]{3,2,1,0:T(8,128)S(1)}, f32[65,8,128]{2,1,0:T(8,128)S(1)}, f32[64,8,128]{2,1,0:T(8,128)S(1)}) custom-call(bf16[8,2,32,8,128]{4,3,2,1,0:T(8,128)(2,1)S(1)} %bitcast.20, bf16[8,2,32,8,128]{4,3,2,1,0:T(8,128)(2,1)S(1)} %collective-permute-done.refs_1_, f32[2,32,8,128]{3,2,1,0:T(8,128)S(1)} %get-tuple-element.42.refs_2_, ...), custom_call_target="tpu_custom_call" | custom-call | tf_op jit(solution)/shard_map/jit(propagate)/propagate/pallas_call | solution.py:147
  28.1 0.7 %collective-permute-done.3 = f16[65,8,128]{2,1,0:T(8,128)(2,1)S(1)} collective-permute-done((f16[65,8,128]{2,1,0:T(8,128)(2,1)S(1)}, f16[65,8,128]{2,1,0:T(8,128)(2,1)S(1)}, u32[]{:S(2)}, u32[]{:S(2)}) %collective-permute-start.3) | collective-permute-done | bytes 133152 | tf_op jit(solution)/shard_map/ppermute | solution.py:301
  28.9 1.5 %propagate.10 = (f32[2,32,8,128]{3,2,1,0:T(8,128)S(1)}, f32[65,8,128]{2,1,0:T(8,128)S(1)}, f32[64,8,128]{2,1,0:T(8,128)S(1)}) custom-call(bf16[8,2,32,8,128]{4,3,2,1,0:T(8,128)(2,1)S(1)} %bitcast.21, bf16[8,2,32,8,128]{4,3,2,1,0:T(8,128)(2,1)S(1)} %collective-permute-done.refs_1_, f32[2,32,8,128]{3,2,1,0:T(8,128)S(1)} %get-tuple-element.31.refs_2_, ...), custom_call_target="tpu_custom_call" | custom-call | tf_op jit(solution)/shard_map/jit(propagate)/propagate/pallas_call | solution.py:147
  30.5 7.4 %collective-permute-done.8 = f16[65,8,128]{2,1,0:T(8,128)(2,1)S(1)} collective-permute-done((f16[65,8,128]{2,1,0:T(8,128)(2,1)S(1)}, f16[65,8,128]{2,1,0:T(8,128)(2,1)S(1)}, u32[]{:S(2)}, u32[]{:S(2)}) %collective-permute-start.8) | collective-permute-done | bytes 133152 | tf_op jit(solution)/shard_map/ppermute | solution.py:301
  37.9 1.5 %propagate.15 = (f32[2,32,8,128]{3,2,1,0:T(8,128)S(1)}, f32[65,8,128]{2,1,0:T(8,128)S(1)}) custom-call(bf16[8,2,32,8,128]{4,3,2,1,0:T(8,128)(2,1)S(1)} %bitcast.22, bf16[8,2,32,8,128]{4,3,2,1,0:T(8,128)(2,1)S(1)} %collective-permute-done.refs_1_, f32[2,32,8,128]{3,2,1,0:T(8,128)S(1)} %get-tuple-element.45.refs_2_, ...), custom_call_target="tpu_custom_call" | custom-call | tf_op jit(solution)/shard_map/jit(propagate)/propagate/pallas_call | solution.py:147
  39.4 0.2 collective-permute-start.9
  39.7 1.5 %propagate.11 = (f32[2,32,8,128]{3,2,1,0:T(8,128)S(1)}, f32[65,8,128]{2,1,0:T(8,128)S(1)}) custom-call(bf16[8,2,32,8,128]{4,3,2,1,0:T(8,128)(2,1)S(1)} %bitcast.23, bf16[8,2,32,8,128]{4,3,2,1,0:T(8,128)(2,1)S(1)} %collective-permute-done.refs_1_, f32[2,32,8,128]{3,2,1,0:T(8,128)S(1)} %get-tuple-element.34.refs_2_, ...), custom_call_target="tpu_custom_call" | custom-call | tf_op jit(solution)/shard_map/jit(propagate)/propagate/pallas_call | solution.py:147
  41.3 7.8 %collective-permute-done.9 = f16[65,8,128]{2,1,0:T(8,128)(2,1)S(1)} collective-permute-done((f16[65,8,128]{2,1,0:T(8,128)(2,1)S(1)}, f16[65,8,128]{2,1,0:T(8,128)(2,1)S(1)}, u32[]{:S(2)}, u32[]{:S(2)}) %collective-permute-start.9) | collective-permute-done | bytes 133152 | tf_op jit(solution)/shard_map/ppermute | solution.py:301
  49.3 1.3 %collective-permute-done.5 = f16[65,8,128]{2,1,0:T(8,128)(2,1)S(1)} collective-permute-done((f16[65,8,128]{2,1,0:T(8,128)(2,1)S(1)}, f16[65,8,128]{2,1,0:T(8,128)(2,1)S(1)}, u32[]{:S(2)}, u32[]{:S(2)}) %collective-permute-start.5) | collective-permute-done | bytes 133152 | tf_op jit(solution)/shard_map/ppermute | solution.py:301
  50.7 1.3 %collective-permute-done.10.refs_2_ = f32[1,32,8,128]{3,2,1,0:T(8,128)S(1)} collective-permute-done((f32[1,32,8,128]{3,2,1,0:T(8,128)S(1)}, f32[1,32,8,128]{3,2,1,0:T(8,128)S(1)}, u32[]{:S(2)}, u32[]{:S(2)}) %collective-permute-start.10) | collective-permute-done | bytes 131104 | tf_op jit(solution)/shard_map/ppermute | solution.py:296
  52.3 8.9 %all_to_all.11 = f32[32,1,128]{2,1,0:T(1,128)S(1)} all-to-all(f32[32,1,128]{2,1,0:T(1,128)S(1)} %bitcast.25), channel_id=1, replica_groups=mesh['seg'=16,'slab'=2] {'seg','slab'}, dimensions={0} | all-to-all | bytes 32768 | tf_op jit(solution)/shard_map/all_to_all | solution.py:363
  61.1 1.1 %solve.1 = f32[4,32,8,128]{3,2,1,0:T(8,128)} custom-call(f32[32,128]{1,0:T(8,128)S(1)} %bitcast.24, f32[1,32,8,128]{3,2,1,0:T(8,128)S(1)} %get-tuple-element.39.refs_0_, f32[1,32,8,128]{3,2,1,0:T(8,128)S(1)} %get-tuple-element.50.refs_1_, f32[1,32,8,128]{3,2,1,0:T(8,128)S(1)} %collective-permute-done.10.refs_2_, ...), custom_call_target="tpu_custom_call" | custom-call | tf_op jit(solution)/shard_map/solve/pallas_call | solution.py:284
  (36 shorter events, 1.3 us)
Async XLA Ops:
  0.0 3.4 %copy-start = (bf16[1,8,2,8,4096]{4,3,2,1,0:T(8,128)(2,1)S(1)}, bf16[1,8,2,8,4096]{4,3,2,1,0:T(8,128)(2,1)}, u32[]{:S(2)}) copy-start(bf16[1,8,2,8,4096]{4,3,2,1,0:T(8,128)(2,1)} %param.3) | copy-start | bytes 3145732
  0.0 3.4 %collective-permute-start = (bf16[8,2,32,8,128]{4,3,2,1,0:T(8,128)(2,1)}, bf16[8,2,32,8,128]{4,3,2,1,0:T(8,128)(2,1)S(1)}, u32[]{:S(2)}, u32[]{:S(2)}) collective-permute-start(bf16[8,2,32,8,128]{4,3,2,1,0:T(8,128)(2,1)} %bitcast.15), channel_id=1, source_target_pairs={{1,0},{0,1},{3,2},{2,3},{5,4},{4,5},{7,6},{6,7},{9,8},{8,9},{11,10... | collective-permute-start | bytes 3145736 | tf_op jit(solution)/shard_map/ppermute | solution.py:296
  1.6 1.8 %collective-permute-start.1 = (f32[2,32,8,128]{3,2,1,0:T(8,128)S(1)}, f32[2,32,8,128]{3,2,1,0:T(8,128)S(1)}, u32[]{:S(2)}, u32[]{:S(2)}) collective-permute-start(f32[2,32,8,128]{3,2,1,0:T(8,128)S(1)} %get-tuple-element.54), channel_id=1, source_target_pairs={{1,0},{0,1},{3,2},{2,3},{5,4},{4,5},{7,6},{6,7},{9,8},{8,9},{11,10... | collective-permute-start | bytes 786440 | tf_op jit(solution)/shard_map/ppermute | solution.py:296
  4.9 10.9 %collective-permute-start.6 = (f16[65,8,128]{2,1,0:T(8,128)(2,1)S(1)}, f16[65,8,128]{2,1,0:T(8,128)(2,1)S(1)}, u32[]{:S(2)}, u32[]{:S(2)}) collective-permute-start(f16[65,8,128]{2,1,0:T(8,128)(2,1)S(1)} %convert_element_type.56), channel_id=1, source_target_pairs={{0,2},{2,4},{4,6},{6,8},{8,10},{10,12},{12,14},{14,16},{16,18},{18... | collective-permute-start | bytes 399368 | tf_op jit(solution)/shard_map/ppermute | solution.py:301
  9.3 9.2 %collective-permute-start.2 = (f16[65,8,128]{2,1,0:T(8,128)(2,1)S(1)}, f16[65,8,128]{2,1,0:T(8,128)(2,1)S(1)}, u32[]{:S(2)}, u32[]{:S(2)}) collective-permute-start(f16[65,8,128]{2,1,0:T(8,128)(2,1)S(1)} %convert_element_type.48), channel_id=1, source_target_pairs={{0,2},{2,4},{4,6},{6,8},{8,10},{10,12},{12,14},{14,16},{16,18},{18... | collective-permute-start | bytes 399368 | tf_op jit(solution)/shard_map/ppermute | solution.py:301
  17.4 9.2 %collective-permute-start.7 = (f16[65,8,128]{2,1,0:T(8,128)(2,1)S(1)}, f16[65,8,128]{2,1,0:T(8,128)(2,1)S(1)}, u32[]{:S(2)}, u32[]{:S(2)}) collective-permute-start(f16[65,8,128]{2,1,0:T(8,128)(2,1)S(1)} %convert_element_type.58), channel_id=1, source_target_pairs={{0,2},{2,4},{4,6},{6,8},{8,10},{10,12},{12,14},{14,16},{16,18},{18... | collective-permute-start | bytes 399368 | tf_op jit(solution)/shard_map/ppermute | solution.py:301
  20.0 8.9 %collective-permute-start.3 = (f16[65,8,128]{2,1,0:T(8,128)(2,1)S(1)}, f16[65,8,128]{2,1,0:T(8,128)(2,1)S(1)}, u32[]{:S(2)}, u32[]{:S(2)}) collective-permute-start(f16[65,8,128]{2,1,0:T(8,128)(2,1)S(1)} %convert_element_type.50), channel_id=1, source_target_pairs={{0,2},{2,4},{4,6},{6,8},{8,10},{10,12},{12,14},{14,16},{16,18},{18... | collective-permute-start | bytes 399368 | tf_op jit(solution)/shard_map/ppermute | solution.py:301
  28.1 9.8 %collective-permute-start.8 = (f16[65,8,128]{2,1,0:T(8,128)(2,1)S(1)}, f16[65,8,128]{2,1,0:T(8,128)(2,1)S(1)}, u32[]{:S(2)}, u32[]{:S(2)}) collective-permute-start(f16[65,8,128]{2,1,0:T(8,128)(2,1)S(1)} %convert_element_type.60), channel_id=1, source_target_pairs={{0,2},{2,4},{4,6},{6,8},{8,10},{10,12},{12,14},{14,16},{16,18},{18... | collective-permute-start | bytes 399368 | tf_op jit(solution)/shard_map/ppermute | solution.py:301
  30.4 9.3 %collective-permute-start.4 = (f16[65,8,128]{2,1,0:T(8,128)(2,1)S(1)}, f16[65,8,128]{2,1,0:T(8,128)(2,1)S(1)}, u32[]{:S(2)}, u32[]{:S(2)}) collective-permute-start(f16[65,8,128]{2,1,0:T(8,128)(2,1)S(1)} %convert_element_type.52), channel_id=1, source_target_pairs={{0,2},{2,4},{4,6},{6,8},{8,10},{10,12},{12,14},{14,16},{16,18},{18... | collective-permute-start | bytes 399368 | tf_op jit(solution)/shard_map/ppermute | solution.py:301
  39.4 9.7 %collective-permute-start.9 = (f16[65,8,128]{2,1,0:T(8,128)(2,1)S(1)}, f16[65,8,128]{2,1,0:T(8,128)(2,1)S(1)}, u32[]{:S(2)}, u32[]{:S(2)}) collective-permute-start(f16[65,8,128]{2,1,0:T(8,128)(2,1)S(1)} %convert_element_type.62), channel_id=1, source_target_pairs={{0,2},{2,4},{4,6},{6,8},{8,10},{10,12},{12,14},{14,16},{16,18},{18... | collective-permute-start | bytes 399368 | tf_op jit(solution)/shard_map/ppermute | solution.py:301
  41.2 9.3 %collective-permute-start.5 = (f16[65,8,128]{2,1,0:T(8,128)(2,1)S(1)}, f16[65,8,128]{2,1,0:T(8,128)(2,1)S(1)}, u32[]{:S(2)}, u32[]{:S(2)}) collective-permute-start(f16[65,8,128]{2,1,0:T(8,128)(2,1)S(1)} %convert_element_type.54), channel_id=1, source_target_pairs={{0,2},{2,4},{4,6},{6,8},{8,10},{10,12},{12,14},{14,16},{16,18},{18... | collective-permute-start | bytes 399368 | tf_op jit(solution)/shard_map/ppermute | solution.py:301
  49.2 1.5 %collective-permute-start.11 = (f32[1,32,8,128]{3,2,1,0:T(8,128)S(1)}, f32[1,32,8,128]{3,2,1,0:T(8,128)S(1)}, u32[]{:S(2)}, u32[]{:S(2)}) collective-permute-start(f32[1,32,8,128]{3,2,1,0:T(8,128)S(1)} %get-tuple-element.52), channel_id=1, source_target_pairs={{1,0},{0,1},{3,2},{2,3},{5,4},{4,5},{7,6},{6,7},{9,8},{8,9},{11,10... | collective-permute-start | bytes 393224 | tf_op jit(solution)/shard_map/ppermute | solution.py:296
  50.7 1.4 %collective-permute-start.10 = (f32[1,32,8,128]{3,2,1,0:T(8,128)S(1)}, f32[1,32,8,128]{3,2,1,0:T(8,128)S(1)}, u32[]{:S(2)}, u32[]{:S(2)}) collective-permute-start(f32[1,32,8,128]{3,2,1,0:T(8,128)S(1)} %get-tuple-element.51), channel_id=1, source_target_pairs={{1,0},{0,1},{3,2},{2,3},{5,4},{4,5},{7,6},{6,7},{9,8},{8,9},{11,10... | collective-permute-start | bytes 393224 | tf_op jit(solution)/shard_map/ppermute | solution.py:296

commit v4 on v3

--- a/solution.py
+++ b/solution.py
@@ -35,10 +35,12 @@
             piece, at = divmod(SUB * b, height)
             rows_at = pl.ds(SUB + SUB * b, SUB)
             here = [source[j % columns, rows_at, :] for j in (-1, 0, 1)]
+            wests = [pltpu.roll(value, 1, 1) for value in here[:2]]
+            easts = [pltpu.roll(value, LANE - 1, 1) for value in here[1:]]
             for j in range(columns):
-                left, centre, right = here
-                west = pltpu.roll(jnp.where(last, left, centre), 1, 1)
-                east = pltpu.roll(jnp.where(first, right, centre), LANE - 1, 1)
+                centre, right = here[1:]
+                west = jnp.where(first, wests[0], wests[1])
+                east = jnp.where(last, easts[1], easts[0])
                 up = source[j, pl.ds(SUB + 1 + SUB * b, SUB), :]
                 down = source[j, pl.ds(SUB - 1 + SUB * b, SUB), :]
                 speed_x = velocity[piece][k, 0, j, pl.ds(at, SUB), :].astype(jnp.float32)
@@ -46,6 +48,9 @@
                 carried = speed_x * (west - east) + speed_y * (down - up)
                 place(target, rows, j, b, 0.9 * centre + ((west + east) + (up + down)) + 0.25 * carried)
                 here = [centre, right, source[(j + 2) % columns, rows_at, :]]
+                if j + 1 < columns:
+                    wests = [wests[1], pltpu.roll(right, 1, 1)]
+                    easts = [easts[1], pltpu.roll(here[2], LANE - 1, 1)]
 
     def pair(i, carry):
         step(2 * i, ping, pong)

time: 62.3 us -> 62.2 us (level)
  transfers between devices with their start and end apart: 12 -> 12, of which waited for: 9 -> 10; matrix products, arithmetic and copies ran while one was open for 2% -> 2% of each run, Pallas kernels for 17% -> 16%
where the time goes in v4:
time: 62.2 us; the launch traced here: 62.1 us
  waiting for transfers between devices  33.2 us (53%)
  Pallas kernels  12.7 us (20%)
  blocking collectives  8.86 us (14%)
  starting transfers between devices  5.6 us (9%)
  local copies, waits for them, and re-layouts  1.1 us (2%)
    ppermute x8, waiting for transfers between devices, to_next(): lax.ppermute(value, 'seg', [(i, (i + 1) % size) for i in range(size)])  30.2 us
    pallas_call x8, Pallas kernels, propagate(): pl.pallas_call(functools.partial(propagate_kernel, pieces, index, first,...  11.4 us
    all_to_all x1, blocking collectives, shards(): gram = lax.all_to_all(gram, ('seg', 'slab'), 0, 0, tiled=True)  8.86 us
    ppermute x8, starting transfers between devices, to_next(): lax.ppermute(value, 'seg', [(i, (i + 1) % size) for i in range(size)])  4.79 us
    ppermute x4, waiting for transfers between devices, from_slab(): lax.ppermute(value, 'slab', [((i + distance) % size, i) for i in range(si...  2.95 us
  transfers between devices with their start and end apart: 12, of which 10 were waited for; matrix products, arithmetic and copies ran while one was open for 2% of the time, Pallas kernels for 16%

profile of v4, /device:TPU:0, one launch (start us, length us, event | category | flops | bytes accessed | tf_op | source)
XLA Modules:
  0.0 62.1 jit_solution(16506672721123544094)
XLA Ops:
  0.0 0.5 collective-permute-start
  0.5 1.1 %dynamic-slice_bitcast_fusion.1 = (f32[2,32,8,128]{3,2,1,0:T(8,128)S(1)}, f32[2,32,8,128]{3,2,1,0:T(8,128)S(1)}) fusion(f32[4,8,32,128]{3,1,2,0:T(8,128)} %bitcast.26, s32[]{:T(128)S(6)} %select_n.6, s32[]{:T(128)S(6)} %select_n.7), kind=kLoop, calls=%fused_computation.3 | loop fusion | bytes 1048584 | tf_op jit(solution)/shard_map/dynamic_slice | solution.py:319
  1.8 1.6 %collective-permute-done.1.refs_3_ = f32[2,32,8,128]{3,2,1,0:T(8,128)S(1)} collective-permute-done((f32[2,32,8,128]{3,2,1,0:T(8,128)S(1)}, f32[2,32,8,128]{3,2,1,0:T(8,128)S(1)}, u32[]{:S(2)}, u32[]{:S(2)}) %collective-permute-start.1) | collective-permute-done | bytes 262176 | tf_op jit(solution)/shard_map/ppermute | solution.py:301
  3.4 1.4 %propagate.12 = (f32[65,8,128]{2,1,0:T(8,128)S(1)}, f32[64,8,128]{2,1,0:T(8,128)S(1)}) custom-call(bf16[8,2,32,8,128]{4,3,2,1,0:T(8,128)(2,1)S(1)} %bitcast.16, bf16[8,2,32,8,128]{4,3,2,1,0:T(8,128)(2,1)S(1)} %collective-permute-done.refs_1_, f32[2,32,8,128]{3,2,1,0:T(8,128)S(1)} %get-tuple-element.53.refs_2_, ...), custom_call_target="tpu_custom_call" | custom-call | tf_op jit(solution)/shard_map/jit(propagate)/propagate/pallas_call | solution.py:152
  4.8 2.9 %collective-permute-start.6 = (f16[65,8,128]{2,1,0:T(8,128)(2,1)S(1)}, f16[65,8,128]{2,1,0:T(8,128)(2,1)S(1)}, u32[]{:S(2)}, u32[]{:S(2)}) collective-permute-start(f16[65,8,128]{2,1,0:T(8,128)(2,1)S(1)} %convert_element_type.56), channel_id=1, source_target_pairs={{0,2},{2,4},{4,6},{6,8},{8,10},{10,12},{12,14},{14,16},{16,18},{18... | collective-permute-start | bytes 399368 | tf_op jit(solution)/shard_map/ppermute | solution.py:306
  7.7 1.4 %propagate.8 = (f32[65,8,128]{2,1,0:T(8,128)S(1)}, f32[64,8,128]{2,1,0:T(8,128)S(1)}) custom-call(bf16[8,2,32,8,128]{4,3,2,1,0:T(8,128)(2,1)S(1)} %bitcast.17, bf16[8,2,32,8,128]{4,3,2,1,0:T(8,128)(2,1)S(1)} %collective-permute-done.refs_1_, f32[2,32,8,128]{3,2,1,0:T(8,128)S(1)} %get-tuple-element.53.refs_2_, ...), custom_call_target="tpu_custom_call" | custom-call | tf_op jit(solution)/shard_map/jit(propagate)/propagate/pallas_call | solution.py:152
  9.2 1.5 %collective-permute-start.2 = (f16[65,8,128]{2,1,0:T(8,128)(2,1)S(1)}, f16[65,8,128]{2,1,0:T(8,128)(2,1)S(1)}, u32[]{:S(2)}, u32[]{:S(2)}) collective-permute-start(f16[65,8,128]{2,1,0:T(8,128)(2,1)S(1)} %convert_element_type.48), channel_id=1, source_target_pairs={{0,2},{2,4},{4,6},{6,8},{8,10},{10,12},{12,14},{14,16},{16,18},{18... | collective-permute-start | bytes 399368 | tf_op jit(solution)/shard_map/ppermute | solution.py:306
  10.7 5.1 %collective-permute-done.6 = f16[65,8,128]{2,1,0:T(8,128)(2,1)S(1)} collective-permute-done((f16[65,8,128]{2,1,0:T(8,128)(2,1)S(1)}, f16[65,8,128]{2,1,0:T(8,128)(2,1)S(1)}, u32[]{:S(2)}, u32[]{:S(2)}) %collective-permute-start.6) | collective-permute-done | bytes 133152 | tf_op jit(solution)/shard_map/ppermute | solution.py:306
  15.8 1.4 %propagate.13 = (f32[2,32,8,128]{3,2,1,0:T(8,128)S(1)}, f32[65,8,128]{2,1,0:T(8,128)S(1)}, f32[64,8,128]{2,1,0:T(8,128)S(1)}) custom-call(bf16[8,2,32,8,128]{4,3,2,1,0:T(8,128)(2,1)S(1)} %bitcast.18, bf16[8,2,32,8,128]{4,3,2,1,0:T(8,128)(2,1)S(1)} %collective-permute-done.refs_1_, f32[2,32,8,128]{3,2,1,0:T(8,128)S(1)} %pad_maximum_fusion.1.refs_2_, ...), custom_call_target="tpu_custom_call" | custom-call | tf_op jit(solution)/shard_map/jit(propagate)/propagate/pallas_call | solution.py:152
  17.4 1.0 %collective-permute-done.2 = f16[65,8,128]{2,1,0:T(8,128)(2,1)S(1)} collective-permute-done((f16[65,8,128]{2,1,0:T(8,128)(2,1)S(1)}, f16[65,8,128]{2,1,0:T(8,128)(2,1)S(1)}, u32[]{:S(2)}, u32[]{:S(2)}) %collective-permute-start.2) | collective-permute-done | bytes 133152 | tf_op jit(solution)/shard_map/ppermute | solution.py:306
  18.4 1.4 %propagate.9 = (f32[2,32,8,128]{3,2,1,0:T(8,128)S(1)}, f32[65,8,128]{2,1,0:T(8,128)S(1)}, f32[64,8,128]{2,1,0:T(8,128)S(1)}) custom-call(bf16[8,2,32,8,128]{4,3,2,1,0:T(8,128)(2,1)S(1)} %bitcast.19, bf16[8,2,32,8,128]{4,3,2,1,0:T(8,128)(2,1)S(1)} %collective-permute-done.refs_1_, f32[2,32,8,128]{3,2,1,0:T(8,128)S(1)} %pad_maximum_fusion.refs_2_, ...), custom_call_target="tpu_custom_call" | custom-call | tf_op jit(solution)/shard_map/jit(propagate)/propagate/pallas_call | solution.py:152
  20.0 6.5 %collective-permute-done.7 = f16[65,8,128]{2,1,0:T(8,128)(2,1)S(1)} collective-permute-done((f16[65,8,128]{2,1,0:T(8,128)(2,1)S(1)}, f16[65,8,128]{2,1,0:T(8,128)(2,1)S(1)}, u32[]{:S(2)}, u32[]{:S(2)}) %collective-permute-start.7) | collective-permute-done | bytes 133152 | tf_op jit(solution)/shard_map/ppermute | solution.py:306
  26.5 1.4 %propagate.14 = (f32[2,32,8,128]{3,2,1,0:T(8,128)S(1)}, f32[65,8,128]{2,1,0:T(8,128)S(1)}, f32[64,8,128]{2,1,0:T(8,128)S(1)}) custom-call(bf16[8,2,32,8,128]{4,3,2,1,0:T(8,128)(2,1)S(1)} %bitcast.20, bf16[8,2,32,8,128]{4,3,2,1,0:T(8,128)(2,1)S(1)} %collective-permute-done.refs_1_, f32[2,32,8,128]{3,2,1,0:T(8,128)S(1)} %get-tuple-element.42.refs_2_, ...), custom_call_target="tpu_custom_call" | custom-call | tf_op jit(solution)/shard_map/jit(propagate)/propagate/pallas_call | solution.py:152
  28.0 0.8 %collective-permute-done.3 = f16[65,8,128]{2,1,0:T(8,128)(2,1)S(1)} collective-permute-done((f16[65,8,128]{2,1,0:T(8,128)(2,1)S(1)}, f16[65,8,128]{2,1,0:T(8,128)(2,1)S(1)}, u32[]{:S(2)}, u32[]{:S(2)}) %collective-permute-start.3) | collective-permute-done | bytes 133152 | tf_op jit(solution)/shard_map/ppermute | solution.py:306
  28.8 1.4 %propagate.10 = (f32[2,32,8,128]{3,2,1,0:T(8,128)S(1)}, f32[65,8,128]{2,1,0:T(8,128)S(1)}, f32[64,8,128]{2,1,0:T(8,128)S(1)}) custom-call(bf16[8,2,32,8,128]{4,3,2,1,0:T(8,128)(2,1)S(1)} %bitcast.21, bf16[8,2,32,8,128]{4,3,2,1,0:T(8,128)(2,1)S(1)} %collective-permute-done.refs_1_, f32[2,32,8,128]{3,2,1,0:T(8,128)S(1)} %get-tuple-element.31.refs_2_, ...), custom_call_target="tpu_custom_call" | custom-call | tf_op jit(solution)/shard_map/jit(propagate)/propagate/pallas_call | solution.py:152
  30.4 7.3 %collective-permute-done.8 = f16[65,8,128]{2,1,0:T(8,128)(2,1)S(1)} collective-permute-done((f16[65,8,128]{2,1,0:T(8,128)(2,1)S(1)}, f16[65,8,128]{2,1,0:T(8,128)(2,1)S(1)}, u32[]{:S(2)}, u32[]{:S(2)}) %collective-permute-start.8) | collective-permute-done | bytes 133152 | tf_op jit(solution)/shard_map/ppermute | solution.py:306
  37.7 1.4 %propagate.15 = (f32[2,32,8,128]{3,2,1,0:T(8,128)S(1)}, f32[65,8,128]{2,1,0:T(8,128)S(1)}) custom-call(bf16[8,2,32,8,128]{4,3,2,1,0:T(8,128)(2,1)S(1)} %bitcast.22, bf16[8,2,32,8,128]{4,3,2,1,0:T(8,128)(2,1)S(1)} %collective-permute-done.refs_1_, f32[2,32,8,128]{3,2,1,0:T(8,128)S(1)} %get-tuple-element.45.refs_2_, ...), custom_call_target="tpu_custom_call" | custom-call | tf_op jit(solution)/shard_map/jit(propagate)/propagate/pallas_call | solution.py:152
  39.3 0.2 collective-permute-done.4
  39.5 1.4 %propagate.11 = (f32[2,32,8,128]{3,2,1,0:T(8,128)S(1)}, f32[65,8,128]{2,1,0:T(8,128)S(1)}) custom-call(bf16[8,2,32,8,128]{4,3,2,1,0:T(8,128)(2,1)S(1)} %bitcast.23, bf16[8,2,32,8,128]{4,3,2,1,0:T(8,128)(2,1)S(1)} %collective-permute-done.refs_1_, f32[2,32,8,128]{3,2,1,0:T(8,128)S(1)} %get-tuple-element.34.refs_2_, ...), custom_call_target="tpu_custom_call" | custom-call | tf_op jit(solution)/shard_map/jit(propagate)/propagate/pallas_call | solution.py:152
  41.0 8.0 %collective-permute-done.9 = f16[65,8,128]{2,1,0:T(8,128)(2,1)S(1)} collective-permute-done((f16[65,8,128]{2,1,0:T(8,128)(2,1)S(1)}, f16[65,8,128]{2,1,0:T(8,128)(2,1)S(1)}, u32[]{:S(2)}, u32[]{:S(2)}) %collective-permute-start.9) | collective-permute-done | bytes 133152 | tf_op jit(solution)/shard_map/ppermute | solution.py:306
  49.2 1.3 %collective-permute-done.5 = f16[65,8,128]{2,1,0:T(8,128)(2,1)S(1)} collective-permute-done((f16[65,8,128]{2,1,0:T(8,128)(2,1)S(1)}, f16[65,8,128]{2,1,0:T(8,128)(2,1)S(1)}, u32[]{:S(2)}, u32[]{:S(2)}) %collective-permute-start.5) | collective-permute-done | bytes 133152 | tf_op jit(solution)/shard_map/ppermute | solution.py:306
  50.6 1.3 %collective-permute-done.10.refs_2_ = f32[1,32,8,128]{3,2,1,0:T(8,128)S(1)} collective-permute-done((f32[1,32,8,128]{3,2,1,0:T(8,128)S(1)}, f32[1,32,8,128]{3,2,1,0:T(8,128)S(1)}, u32[]{:S(2)}, u32[]{:S(2)}) %collective-permute-start.10) | collective-permute-done | bytes 131104 | tf_op jit(solution)/shard_map/ppermute | solution.py:301
  52.1 8.9 %all_to_all.11 = f32[32,1,128]{2,1,0:T(1,128)S(1)} all-to-all(f32[32,1,128]{2,1,0:T(1,128)S(1)} %bitcast.25), channel_id=1, replica_groups=mesh['seg'=16,'slab'=2] {'seg','slab'}, dimensions={0} | all-to-all | bytes 32768 | tf_op jit(solution)/shard_map/all_to_all | solution.py:368
  61.0 1.1 %solve.1 = f32[4,32,8,128]{3,2,1,0:T(8,128)} custom-call(f32[32,128]{1,0:T(8,128)S(1)} %bitcast.24, f32[1,32,8,128]{3,2,1,0:T(8,128)S(1)} %get-tuple-element.39.refs_0_, f32[1,32,8,128]{3,2,1,0:T(8,128)S(1)} %get-tuple-element.50.refs_1_, f32[1,32,8,128]{3,2,1,0:T(8,128)S(1)} %collective-permute-done.10.refs_2_, ...), custom_call_target="tpu_custom_call" | custom-call | tf_op jit(solution)/shard_map/solve/pallas_call | solution.py:289
  (36 shorter events, 1.4 us)
Async XLA Ops:
  0.0 3.4 %copy-start = (bf16[1,8,2,8,4096]{4,3,2,1,0:T(8,128)(2,1)S(1)}, bf16[1,8,2,8,4096]{4,3,2,1,0:T(8,128)(2,1)}, u32[]{:S(2)}) copy-start(bf16[1,8,2,8,4096]{4,3,2,1,0:T(8,128)(2,1)} %param.3) | copy-start | bytes 3145732
  0.0 3.4 %collective-permute-start = (bf16[8,2,32,8,128]{4,3,2,1,0:T(8,128)(2,1)}, bf16[8,2,32,8,128]{4,3,2,1,0:T(8,128)(2,1)S(1)}, u32[]{:S(2)}, u32[]{:S(2)}) collective-permute-start(bf16[8,2,32,8,128]{4,3,2,1,0:T(8,128)(2,1)} %bitcast.15), channel_id=1, source_target_pairs={{1,0},{0,1},{3,2},{2,3},{5,4},{4,5},{7,6},{6,7},{9,8},{8,9},{11,10... | collective-permute-start | bytes 3145736 | tf_op jit(solution)/shard_map/ppermute | solution.py:301
  1.6 1.8 %collective-permute-start.1 = (f32[2,32,8,128]{3,2,1,0:T(8,128)S(1)}, f32[2,32,8,128]{3,2,1,0:T(8,128)S(1)}, u32[]{:S(2)}, u32[]{:S(2)}) collective-permute-start(f32[2,32,8,128]{3,2,1,0:T(8,128)S(1)} %get-tuple-element.54), channel_id=1, source_target_pairs={{1,0},{0,1},{3,2},{2,3},{5,4},{4,5},{7,6},{6,7},{9,8},{8,9},{11,10... | collective-permute-start | bytes 786440 | tf_op jit(solution)/shard_map/ppermute | solution.py:301
  4.8 11.0 %collective-permute-start.6 = (f16[65,8,128]{2,1,0:T(8,128)(2,1)S(1)}, f16[65,8,128]{2,1,0:T(8,128)(2,1)S(1)}, u32[]{:S(2)}, u32[]{:S(2)}) collective-permute-start(f16[65,8,128]{2,1,0:T(8,128)(2,1)S(1)} %convert_element_type.56), channel_id=1, source_target_pairs={{0,2},{2,4},{4,6},{6,8},{8,10},{10,12},{12,14},{14,16},{16,18},{18... | collective-permute-start | bytes 399368 | tf_op jit(solution)/shard_map/ppermute | solution.py:306
  9.2 9.2 %collective-permute-start.2 = (f16[65,8,128]{2,1,0:T(8,128)(2,1)S(1)}, f16[65,8,128]{2,1,0:T(8,128)(2,1)S(1)}, u32[]{:S(2)}, u32[]{:S(2)}) collective-permute-start(f16[65,8,128]{2,1,0:T(8,128)(2,1)S(1)} %convert_element_type.48), channel_id=1, source_target_pairs={{0,2},{2,4},{4,6},{6,8},{8,10},{10,12},{12,14},{14,16},{16,18},{18... | collective-permute-start | bytes 399368 | tf_op jit(solution)/shard_map/ppermute | solution.py:306
  17.3 9.2 %collective-permute-start.7 = (f16[65,8,128]{2,1,0:T(8,128)(2,1)S(1)}, f16[65,8,128]{2,1,0:T(8,128)(2,1)S(1)}, u32[]{:S(2)}, u32[]{:S(2)}) collective-permute-start(f16[65,8,128]{2,1,0:T(8,128)(2,1)S(1)} %convert_element_type.58), channel_id=1, source_target_pairs={{0,2},{2,4},{4,6},{6,8},{8,10},{10,12},{12,14},{14,16},{16,18},{18... | collective-permute-start | bytes 399368 | tf_op jit(solution)/shard_map/ppermute | solution.py:306
  19.9 8.9 %collective-permute-start.3 = (f16[65,8,128]{2,1,0:T(8,128)(2,1)S(1)}, f16[65,8,128]{2,1,0:T(8,128)(2,1)S(1)}, u32[]{:S(2)}, u32[]{:S(2)}) collective-permute-start(f16[65,8,128]{2,1,0:T(8,128)(2,1)S(1)} %convert_element_type.50), channel_id=1, source_target_pairs={{0,2},{2,4},{4,6},{6,8},{8,10},{10,12},{12,14},{14,16},{16,18},{18... | collective-permute-start | bytes 399368 | tf_op jit(solution)/shard_map/ppermute | solution.py:306
  28.0 9.7 %collective-permute-start.8 = (f16[65,8,128]{2,1,0:T(8,128)(2,1)S(1)}, f16[65,8,128]{2,1,0:T(8,128)(2,1)S(1)}, u32[]{:S(2)}, u32[]{:S(2)}) collective-permute-start(f16[65,8,128]{2,1,0:T(8,128)(2,1)S(1)} %convert_element_type.60), channel_id=1, source_target_pairs={{0,2},{2,4},{4,6},{6,8},{8,10},{10,12},{12,14},{14,16},{16,18},{18... | collective-permute-start | bytes 399368 | tf_op jit(solution)/shard_map/ppermute | solution.py:306
  30.3 9.2 %collective-permute-start.4 = (f16[65,8,128]{2,1,0:T(8,128)(2,1)S(1)}, f16[65,8,128]{2,1,0:T(8,128)(2,1)S(1)}, u32[]{:S(2)}, u32[]{:S(2)}) collective-permute-start(f16[65,8,128]{2,1,0:T(8,128)(2,1)S(1)} %convert_element_type.52), channel_id=1, source_target_pairs={{0,2},{2,4},{4,6},{6,8},{8,10},{10,12},{12,14},{14,16},{16,18},{18... | collective-permute-start | bytes 399368 | tf_op jit(solution)/shard_map/ppermute | solution.py:306
  39.2 9.9 %collective-permute-start.9 = (f16[65,8,128]{2,1,0:T(8,128)(2,1)S(1)}, f16[65,8,128]{2,1,0:T(8,128)(2,1)S(1)}, u32[]{:S(2)}, u32[]{:S(2)}) collective-permute-start(f16[65,8,128]{2,1,0:T(8,128)(2,1)S(1)} %convert_element_type.62), channel_id=1, source_target_pairs={{0,2},{2,4},{4,6},{6,8},{8,10},{10,12},{12,14},{14,16},{16,18},{18... | collective-permute-start | bytes 399368 | tf_op jit(solution)/shard_map/ppermute | solution.py:306
  40.9 9.5 %collective-permute-start.5 = (f16[65,8,128]{2,1,0:T(8,128)(2,1)S(1)}, f16[65,8,128]{2,1,0:T(8,128)(2,1)S(1)}, u32[]{:S(2)}, u32[]{:S(2)}) collective-permute-start(f16[65,8,128]{2,1,0:T(8,128)(2,1)S(1)} %convert_element_type.54), channel_id=1, source_target_pairs={{0,2},{2,4},{4,6},{6,8},{8,10},{10,12},{12,14},{14,16},{16,18},{18... | collective-permute-start | bytes 399368 | tf_op jit(solution)/shard_map/ppermute | solution.py:306
  49.1 1.5 %collective-permute-start.11 = (f32[1,32,8,128]{3,2,1,0:T(8,128)S(1)}, f32[1,32,8,128]{3,2,1,0:T(8,128)S(1)}, u32[]{:S(2)}, u32[]{:S(2)}) collective-permute-start(f32[1,32,8,128]{3,2,1,0:T(8,128)S(1)} %get-tuple-element.52), channel_id=1, source_target_pairs={{1,0},{0,1},{3,2},{2,3},{5,4},{4,5},{7,6},{6,7},{9,8},{8,9},{11,10... | collective-permute-start | bytes 393224 | tf_op jit(solution)/shard_map/ppermute | solution.py:301
  50.5 1.4 %collective-permute-start.10 = (f32[1,32,8,128]{3,2,1,0:T(8,128)S(1)}, f32[1,32,8,128]{3,2,1,0:T(8,128)S(1)}, u32[]{:S(2)}, u32[]{:S(2)}) collective-permute-start(f32[1,32,8,128]{3,2,1,0:T(8,128)S(1)} %get-tuple-element.51), channel_id=1, source_target_pairs={{1,0},{0,1},{3,2},{2,3},{5,4},{4,5},{7,6},{6,7},{9,8},{8,9},{11,10... | collective-permute-start | bytes 393224 | tf_op jit(solution)/shard_map/ppermute | solution.py:301

commit v5 on v4

--- a/solution.py
+++ b/solution.py
@@ -248,7 +248,7 @@
 
 
 def solve_kernel(share, gram, *refs):
-    residual, out = refs[:-1], refs[-1]
+    residual, (target, out, done) = refs[:-3], refs[-3:]
     count, columns, height, lane = out.shape
     line = jnp.broadcast_to(jnp.sum(gram[...], axis=0, keepdims=True), (count * count, lane))
     total = jnp.sum(jnp.where(diagonal(count), line, 0.0), axis=1, keepdims=True)
@@ -269,6 +269,12 @@
             inverse[a, b] = -value / lower[a, a]
     factors = {at: jnp.broadcast_to(value, (SUB, lane)) for at, value in inverse.items()}
 
+    part = columns // done.shape[0]
+
+    def copy(q):
+        some = pl.ds(q * part, part)
+        return pltpu.make_async_copy(out.at[:, some], target.at[:, some], done.at[q])
+
     def finish(place):
         for j in range(columns):
             for at in range(0, height, SUB):
@@ -278,6 +284,10 @@
                     for b in range(1, a + 1):
                         value = value + factors[a, b] * values[b]
                     out[a, j, pl.ds(at, SUB), :] = value
+            if (j + 1) % part == 0:
+                copy(j // part).start()
+        for q in range(columns // part):
+            copy(q).wait()
 
     base = lax.axis_index("slab") * share
     for turn in range(0, count, share or count):
@@ -286,11 +296,16 @@
 
 def solved(share, gram, residual):
     count, (_, columns, height, lane) = len(residual), residual[0].shape
+    quarters = 4 if columns % 4 == 0 else 1
     return pl.pallas_call(
         functools.partial(solve_kernel, share),
         out_shape=jax.ShapeDtypeStruct((count, columns, height, lane), jnp.float32),
         in_specs=[VMEM] * (1 + count),
-        out_specs=VMEM,
+        out_specs=pl.BlockSpec(memory_space=pl.ANY),
+        scratch_shapes=[
+            pltpu.VMEM((count, columns, height, lane), jnp.float32),
+            pltpu.SemaphoreType.DMA((quarters,)),
+        ],
         compiler_params=pltpu.CompilerParams(vmem_limit_bytes=16 << 20),
         name="solve",
     )(gram, *residual)

time: 62.2 us -> 62.4 us (level)
  transfers between devices with their start and end apart: 12 -> 12, of which waited for: 10 -> 9; matrix products, arithmetic and copies ran while one was open for 2% -> 2% of each run, Pallas kernels for 16% -> 16%
where the time goes in v5:
time: 62.4 us; the launch traced here: 62.2 us
  waiting for transfers between devices  33 us (53%)
  Pallas kernels  12.7 us (20%)
  blocking collectives  8.86 us (14%)
  starting transfers between devices  5.78 us (9%)
  local copies, waits for them, and re-layouts  1.1 us (2%)
    ppermute x8, waiting for transfers between devices, to_next(): lax.ppermute(value, 'seg', [(i, (i + 1) % size) for i in range(size)])  30.1 us
    pallas_call x8, Pallas kernels, propagate(): pl.pallas_call(functools.partial(propagate_kernel, pieces, index, first,...  11.4 us
    all_to_all x1, blocking collectives, shards(): gram = lax.all_to_all(gram, ('seg', 'slab'), 0, 0, tiled=True)  8.86 us
    ppermute x8, starting transfers between devices, to_next(): lax.ppermute(value, 'seg', [(i, (i + 1) % size) for i in range(size)])  4.98 us
    ppermute x4, waiting for transfers between devices, from_slab(): lax.ppermute(value, 'slab', [((i + distance) % size, i) for i in range(si...  2.95 us
  transfers between devices with their start and end apart: 12, of which 9 were waited for; matrix products, arithmetic and copies ran while one was open for 2% of the time, Pallas kernels for 16%

profile of v5, /device:TPU:0, one launch (start us, length us, event | category | flops | bytes accessed | tf_op | source)
XLA Modules:
  0.0 62.2 jit_solution(6844630422122122794)
XLA Ops:
  0.0 0.5 collective-permute-start
  0.5 1.1 %dynamic-slice_bitcast_fusion.1 = (f32[2,32,8,128]{3,2,1,0:T(8,128)S(1)}, f32[2,32,8,128]{3,2,1,0:T(8,128)S(1)}) fusion(f32[4,8,32,128]{3,1,2,0:T(8,128)} %bitcast.26, s32[]{:T(128)S(6)} %select_n.6, s32[]{:T(128)S(6)} %select_n.7), kind=kLoop, calls=%fused_computation.3 | loop fusion | bytes 1048584 | tf_op jit(solution)/shard_map/dynamic_slice | solution.py:334
  1.8 1.6 %collective-permute-done.1.refs_3_ = f32[2,32,8,128]{3,2,1,0:T(8,128)S(1)} collective-permute-done((f32[2,32,8,128]{3,2,1,0:T(8,128)S(1)}, f32[2,32,8,128]{3,2,1,0:T(8,128)S(1)}, u32[]{:S(2)}, u32[]{:S(2)}) %collective-permute-start.1) | collective-permute-done | bytes 262176 | tf_op jit(solution)/shard_map/ppermute | solution.py:316
  3.4 1.4 %propagate.12 = (f32[65,8,128]{2,1,0:T(8,128)S(1)}, f32[64,8,128]{2,1,0:T(8,128)S(1)}) custom-call(bf16[8,2,32,8,128]{4,3,2,1,0:T(8,128)(2,1)S(1)} %bitcast.16, bf16[8,2,32,8,128]{4,3,2,1,0:T(8,128)(2,1)S(1)} %collective-permute-done.refs_1_, f32[2,32,8,128]{3,2,1,0:T(8,128)S(1)} %get-tuple-element.53.refs_2_, ...), custom_call_target="tpu_custom_call" | custom-call | tf_op jit(solution)/shard_map/jit(propagate)/propagate/pallas_call | solution.py:152
  4.8 2.9 %collective-permute-start.6 = (f16[65,8,128]{2,1,0:T(8,128)(2,1)S(1)}, f16[65,8,128]{2,1,0:T(8,128)(2,1)S(1)}, u32[]{:S(2)}, u32[]{:S(2)}) collective-permute-start(f16[65,8,128]{2,1,0:T(8,128)(2,1)S(1)} %convert_element_type.56), channel_id=1, source_target_pairs={{0,2},{2,4},{4,6},{6,8},{8,10},{10,12},{12,14},{14,16},{16,18},{18... | collective-permute-start | bytes 399368 | tf_op jit(solution)/shard_map/ppermute | solution.py:321
  7.7 1.4 %propagate.8 = (f32[65,8,128]{2,1,0:T(8,128)S(1)}, f32[64,8,128]{2,1,0:T(8,128)S(1)}) custom-call(bf16[8,2,32,8,128]{4,3,2,1,0:T(8,128)(2,1)S(1)} %bitcast.17, bf16[8,2,32,8,128]{4,3,2,1,0:T(8,128)(2,1)S(1)} %collective-permute-done.refs_1_, f32[2,32,8,128]{3,2,1,0:T(8,128)S(1)} %get-tuple-element.53.refs_2_, ...), custom_call_target="tpu_custom_call" | custom-call | tf_op jit(solution)/shard_map/jit(propagate)/propagate/pallas_call | solution.py:152
  9.2 1.5 %collective-permute-start.2 = (f16[65,8,128]{2,1,0:T(8,128)(2,1)S(1)}, f16[65,8,128]{2,1,0:T(8,128)(2,1)S(1)}, u32[]{:S(2)}, u32[]{:S(2)}) collective-permute-start(f16[65,8,128]{2,1,0:T(8,128)(2,1)S(1)} %convert_element_type.48), channel_id=1, source_target_pairs={{0,2},{2,4},{4,6},{6,8},{8,10},{10,12},{12,14},{14,16},{16,18},{18... | collective-permute-start | bytes 399368 | tf_op jit(solution)/shard_map/ppermute | solution.py:321
  10.7 5.1 %collective-permute-done.6 = f16[65,8,128]{2,1,0:T(8,128)(2,1)S(1)} collective-permute-done((f16[65,8,128]{2,1,0:T(8,128)(2,1)S(1)}, f16[65,8,128]{2,1,0:T(8,128)(2,1)S(1)}, u32[]{:S(2)}, u32[]{:S(2)}) %collective-permute-start.6) | collective-permute-done | bytes 133152 | tf_op jit(solution)/shard_map/ppermute | solution.py:321
  15.8 1.4 %propagate.13 = (f32[2,32,8,128]{3,2,1,0:T(8,128)S(1)}, f32[65,8,128]{2,1,0:T(8,128)S(1)}, f32[64,8,128]{2,1,0:T(8,128)S(1)}) custom-call(bf16[8,2,32,8,128]{4,3,2,1,0:T(8,128)(2,1)S(1)} %bitcast.18, bf16[8,2,32,8,128]{4,3,2,1,0:T(8,128)(2,1)S(1)} %collective-permute-done.refs_1_, f32[2,32,8,128]{3,2,1,0:T(8,128)S(1)} %pad_maximum_fusion.1.refs_2_, ...), custom_call_target="tpu_custom_call" | custom-call | tf_op jit(solution)/shard_map/jit(propagate)/propagate/pallas_call | solution.py:152
  17.4 1.0 %collective-permute-done.2 = f16[65,8,128]{2,1,0:T(8,128)(2,1)S(1)} collective-permute-done((f16[65,8,128]{2,1,0:T(8,128)(2,1)S(1)}, f16[65,8,128]{2,1,0:T(8,128)(2,1)S(1)}, u32[]{:S(2)}, u32[]{:S(2)}) %collective-permute-start.2) | collective-permute-done | bytes 133152 | tf_op jit(solution)/shard_map/ppermute | solution.py:321
  18.4 1.4 %propagate.9 = (f32[2,32,8,128]{3,2,1,0:T(8,128)S(1)}, f32[65,8,128]{2,1,0:T(8,128)S(1)}, f32[64,8,128]{2,1,0:T(8,128)S(1)}) custom-call(bf16[8,2,32,8,128]{4,3,2,1,0:T(8,128)(2,1)S(1)} %bitcast.19, bf16[8,2,32,8,128]{4,3,2,1,0:T(8,128)(2,1)S(1)} %collective-permute-done.refs_1_, f32[2,32,8,128]{3,2,1,0:T(8,128)S(1)} %pad_maximum_fusion.refs_2_, ...), custom_call_target="tpu_custom_call" | custom-call | tf_op jit(solution)/shard_map/jit(propagate)/propagate/pallas_call | solution.py:152
  20.0 6.5 %collective-permute-done.7 = f16[65,8,128]{2,1,0:T(8,128)(2,1)S(1)} collective-permute-done((f16[65,8,128]{2,1,0:T(8,128)(2,1)S(1)}, f16[65,8,128]{2,1,0:T(8,128)(2,1)S(1)}, u32[]{:S(2)}, u32[]{:S(2)}) %collective-permute-start.7) | collective-permute-done | bytes 133152 | tf_op jit(solution)/shard_map/ppermute | solution.py:321
  26.5 1.4 %propagate.14 = (f32[2,32,8,128]{3,2,1,0:T(8,128)S(1)}, f32[65,8,128]{2,1,0:T(8,128)S(1)}, f32[64,8,128]{2,1,0:T(8,128)S(1)}) custom-call(bf16[8,2,32,8,128]{4,3,2,1,0:T(8,128)(2,1)S(1)} %bitcast.20, bf16[8,2,32,8,128]{4,3,2,1,0:T(8,128)(2,1)S(1)} %collective-permute-done.refs_1_, f32[2,32,8,128]{3,2,1,0:T(8,128)S(1)} %get-tuple-element.42.refs_2_, ...), custom_call_target="tpu_custom_call" | custom-call | tf_op jit(solution)/shard_map/jit(propagate)/propagate/pallas_call | solution.py:152
  28.0 0.8 %collective-permute-done.3 = f16[65,8,128]{2,1,0:T(8,128)(2,1)S(1)} collective-permute-done((f16[65,8,128]{2,1,0:T(8,128)(2,1)S(1)}, f16[65,8,128]{2,1,0:T(8,128)(2,1)S(1)}, u32[]{:S(2)}, u32[]{:S(2)}) %collective-permute-start.3) | collective-permute-done | bytes 133152 | tf_op jit(solution)/shard_map/ppermute | solution.py:321
  28.8 1.4 %propagate.10 = (f32[2,32,8,128]{3,2,1,0:T(8,128)S(1)}, f32[65,8,128]{2,1,0:T(8,128)S(1)}, f32[64,8,128]{2,1,0:T(8,128)S(1)}) custom-call(bf16[8,2,32,8,128]{4,3,2,1,0:T(8,128)(2,1)S(1)} %bitcast.21, bf16[8,2,32,8,128]{4,3,2,1,0:T(8,128)(2,1)S(1)} %collective-permute-done.refs_1_, f32[2,32,8,128]{3,2,1,0:T(8,128)S(1)} %get-tuple-element.31.refs_2_, ...), custom_call_target="tpu_custom_call" | custom-call | tf_op jit(solution)/shard_map/jit(propagate)/propagate/pallas_call | solution.py:152
  30.4 7.3 %collective-permute-done.8 = f16[65,8,128]{2,1,0:T(8,128)(2,1)S(1)} collective-permute-done((f16[65,8,128]{2,1,0:T(8,128)(2,1)S(1)}, f16[65,8,128]{2,1,0:T(8,128)(2,1)S(1)}, u32[]{:S(2)}, u32[]{:S(2)}) %collective-permute-start.8) | collective-permute-done | bytes 133152 | tf_op jit(solution)/shard_map/ppermute | solution.py:321
  37.7 1.4 %propagate.15 = (f32[2,32,8,128]{3,2,1,0:T(8,128)S(1)}, f32[65,8,128]{2,1,0:T(8,128)S(1)}) custom-call(bf16[8,2,32,8,128]{4,3,2,1,0:T(8,128)(2,1)S(1)} %bitcast.22, bf16[8,2,32,8,128]{4,3,2,1,0:T(8,128)(2,1)S(1)} %collective-permute-done.refs_1_, f32[2,32,8,128]{3,2,1,0:T(8,128)S(1)} %get-tuple-element.45.refs_2_, ...), custom_call_target="tpu_custom_call" | custom-call | tf_op jit(solution)/shard_map/jit(propagate)/propagate/pallas_call | solution.py:152
  39.2 0.2 collective-permute-start.9
  39.5 1.4 %propagate.11 = (f32[2,32,8,128]{3,2,1,0:T(8,128)S(1)}, f32[65,8,128]{2,1,0:T(8,128)S(1)}) custom-call(bf16[8,2,32,8,128]{4,3,2,1,0:T(8,128)(2,1)S(1)} %bitcast.23, bf16[8,2,32,8,128]{4,3,2,1,0:T(8,128)(2,1)S(1)} %collective-permute-done.refs_1_, f32[2,32,8,128]{3,2,1,0:T(8,128)S(1)} %get-tuple-element.34.refs_2_, ...), custom_call_target="tpu_custom_call" | custom-call | tf_op jit(solution)/shard_map/jit(propagate)/propagate/pallas_call | solution.py:152
  41.0 8.0 %collective-permute-done.9 = f16[65,8,128]{2,1,0:T(8,128)(2,1)S(1)} collective-permute-done((f16[65,8,128]{2,1,0:T(8,128)(2,1)S(1)}, f16[65,8,128]{2,1,0:T(8,128)(2,1)S(1)}, u32[]{:S(2)}, u32[]{:S(2)}) %collective-permute-start.9) | collective-permute-done | bytes 133152 | tf_op jit(solution)/shard_map/ppermute | solution.py:321
  49.2 1.3 %collective-permute-done.5 = f16[65,8,128]{2,1,0:T(8,128)(2,1)S(1)} collective-permute-done((f16[65,8,128]{2,1,0:T(8,128)(2,1)S(1)}, f16[65,8,128]{2,1,0:T(8,128)(2,1)S(1)}, u32[]{:S(2)}, u32[]{:S(2)}) %collective-permute-start.5) | collective-permute-done | bytes 133152 | tf_op jit(solution)/shard_map/ppermute | solution.py:321
  50.6 1.3 %collective-permute-done.10.refs_2_ = f32[1,32,8,128]{3,2,1,0:T(8,128)S(1)} collective-permute-done((f32[1,32,8,128]{3,2,1,0:T(8,128)S(1)}, f32[1,32,8,128]{3,2,1,0:T(8,128)S(1)}, u32[]{:S(2)}, u32[]{:S(2)}) %collective-permute-start.10) | collective-permute-done | bytes 131104 | tf_op jit(solution)/shard_map/ppermute | solution.py:316
  52.1 8.9 %all_to_all.11 = f32[32,1,128]{2,1,0:T(1,128)S(1)} all-to-all(f32[32,1,128]{2,1,0:T(1,128)S(1)} %bitcast.25), channel_id=1, replica_groups=mesh['seg'=16,'slab'=2] {'seg','slab'}, dimensions={0} | all-to-all | bytes 32768 | tf_op jit(solution)/shard_map/all_to_all | solution.py:383
  61.0 1.0 %solve.1 = f32[4,32,8,128]{3,2,1,0:T(8,128)} custom-call(f32[32,128]{1,0:T(8,128)S(1)} %bitcast.24, f32[1,32,8,128]{3,2,1,0:T(8,128)S(1)} %get-tuple-element.39.refs_0_, f32[1,32,8,128]{3,2,1,0:T(8,128)S(1)} %get-tuple-element.50.refs_1_, f32[1,32,8,128]{3,2,1,0:T(8,128)S(1)} %collective-permute-done.10.refs_2_, ...), custom_call_target="tpu_custom_call" | custom-call | tf_op jit(solution)/shard_map/solve/pallas_call | solution.py:300
  (36 shorter events, 1.3 us)
Async XLA Ops:
  0.0 3.4 %copy-start = (bf16[1,8,2,8,4096]{4,3,2,1,0:T(8,128)(2,1)S(1)}, bf16[1,8,2,8,4096]{4,3,2,1,0:T(8,128)(2,1)}, u32[]{:S(2)}) copy-start(bf16[1,8,2,8,4096]{4,3,2,1,0:T(8,128)(2,1)} %param.3) | copy-start | bytes 3145732
  0.0 3.4 %collective-permute-start = (bf16[8,2,32,8,128]{4,3,2,1,0:T(8,128)(2,1)}, bf16[8,2,32,8,128]{4,3,2,1,0:T(8,128)(2,1)S(1)}, u32[]{:S(2)}, u32[]{:S(2)}) collective-permute-start(bf16[8,2,32,8,128]{4,3,2,1,0:T(8,128)(2,1)} %bitcast.15), channel_id=1, source_target_pairs={{1,0},{0,1},{3,2},{2,3},{5,4},{4,5},{7,6},{6,7},{9,8},{8,9},{11,10... | collective-permute-start | bytes 3145736 | tf_op jit(solution)/shard_map/ppermute | solution.py:316
  1.6 1.8 %collective-permute-start.1 = (f32[2,32,8,128]{3,2,1,0:T(8,128)S(1)}, f32[2,32,8,128]{3,2,1,0:T(8,128)S(1)}, u32[]{:S(2)}, u32[]{:S(2)}) collective-permute-start(f32[2,32,8,128]{3,2,1,0:T(8,128)S(1)} %get-tuple-element.54), channel_id=1, source_target_pairs={{1,0},{0,1},{3,2},{2,3},{5,4},{4,5},{7,6},{6,7},{9,8},{8,9},{11,10... | collective-permute-start | bytes 786440 | tf_op jit(solution)/shard_map/ppermute | solution.py:316
  4.8 11.0 %collective-permute-start.6 = (f16[65,8,128]{2,1,0:T(8,128)(2,1)S(1)}, f16[65,8,128]{2,1,0:T(8,128)(2,1)S(1)}, u32[]{:S(2)}, u32[]{:S(2)}) collective-permute-start(f16[65,8,128]{2,1,0:T(8,128)(2,1)S(1)} %convert_element_type.56), channel_id=1, source_target_pairs={{0,2},{2,4},{4,6},{6,8},{8,10},{10,12},{12,14},{14,16},{16,18},{18... | collective-permute-start | bytes 399368 | tf_op jit(solution)/shard_map/ppermute | solution.py:321
  9.2 9.2 %collective-permute-start.2 = (f16[65,8,128]{2,1,0:T(8,128)(2,1)S(1)}, f16[65,8,128]{2,1,0:T(8,128)(2,1)S(1)}, u32[]{:S(2)}, u32[]{:S(2)}) collective-permute-start(f16[65,8,128]{2,1,0:T(8,128)(2,1)S(1)} %convert_element_type.48), channel_id=1, source_target_pairs={{0,2},{2,4},{4,6},{6,8},{8,10},{10,12},{12,14},{14,16},{16,18},{18... | collective-permute-start | bytes 399368 | tf_op jit(solution)/shard_map/ppermute | solution.py:321
  17.3 9.2 %collective-permute-start.7 = (f16[65,8,128]{2,1,0:T(8,128)(2,1)S(1)}, f16[65,8,128]{2,1,0:T(8,128)(2,1)S(1)}, u32[]{:S(2)}, u32[]{:S(2)}) collective-permute-start(f16[65,8,128]{2,1,0:T(8,128)(2,1)S(1)} %convert_element_type.58), channel_id=1, source_target_pairs={{0,2},{2,4},{4,6},{6,8},{8,10},{10,12},{12,14},{14,16},{16,18},{18... | collective-permute-start | bytes 399368 | tf_op jit(solution)/shard_map/ppermute | solution.py:321
  19.9 8.9 %collective-permute-start.3 = (f16[65,8,128]{2,1,0:T(8,128)(2,1)S(1)}, f16[65,8,128]{2,1,0:T(8,128)(2,1)S(1)}, u32[]{:S(2)}, u32[]{:S(2)}) collective-permute-start(f16[65,8,128]{2,1,0:T(8,128)(2,1)S(1)} %convert_element_type.50), channel_id=1, source_target_pairs={{0,2},{2,4},{4,6},{6,8},{8,10},{10,12},{12,14},{14,16},{16,18},{18... | collective-permute-start | bytes 399368 | tf_op jit(solution)/shard_map/ppermute | solution.py:321
  28.0 9.7 %collective-permute-start.8 = (f16[65,8,128]{2,1,0:T(8,128)(2,1)S(1)}, f16[65,8,128]{2,1,0:T(8,128)(2,1)S(1)}, u32[]{:S(2)}, u32[]{:S(2)}) collective-permute-start(f16[65,8,128]{2,1,0:T(8,128)(2,1)S(1)} %convert_element_type.60), channel_id=1, source_target_pairs={{0,2},{2,4},{4,6},{6,8},{8,10},{10,12},{12,14},{14,16},{16,18},{18... | collective-permute-start | bytes 399368 | tf_op jit(solution)/shard_map/ppermute | solution.py:321
  30.3 9.2 %collective-permute-start.4 = (f16[65,8,128]{2,1,0:T(8,128)(2,1)S(1)}, f16[65,8,128]{2,1,0:T(8,128)(2,1)S(1)}, u32[]{:S(2)}, u32[]{:S(2)}) collective-permute-start(f16[65,8,128]{2,1,0:T(8,128)(2,1)S(1)} %convert_element_type.52), channel_id=1, source_target_pairs={{0,2},{2,4},{4,6},{6,8},{8,10},{10,12},{12,14},{14,16},{16,18},{18... | collective-permute-start | bytes 399368 | tf_op jit(solution)/shard_map/ppermute | solution.py:321
  39.2 9.9 %collective-permute-start.9 = (f16[65,8,128]{2,1,0:T(8,128)(2,1)S(1)}, f16[65,8,128]{2,1,0:T(8,128)(2,1)S(1)}, u32[]{:S(2)}, u32[]{:S(2)}) collective-permute-start(f16[65,8,128]{2,1,0:T(8,128)(2,1)S(1)} %convert_element_type.62), channel_id=1, source_target_pairs={{0,2},{2,4},{4,6},{6,8},{8,10},{10,12},{12,14},{14,16},{16,18},{18... | collective-permute-start | bytes 399368 | tf_op jit(solution)/shard_map/ppermute | solution.py:321
  40.9 9.5 %collective-permute-start.5 = (f16[65,8,128]{2,1,0:T(8,128)(2,1)S(1)}, f16[65,8,128]{2,1,0:T(8,128)(2,1)S(1)}, u32[]{:S(2)}, u32[]{:S(2)}) collective-permute-start(f16[65,8,128]{2,1,0:T(8,128)(2,1)S(1)} %convert_element_type.54), channel_id=1, source_target_pairs={{0,2},{2,4},{4,6},{6,8},{8,10},{10,12},{12,14},{14,16},{16,18},{18... | collective-permute-start | bytes 399368 | tf_op jit(solution)/shard_map/ppermute | solution.py:321
  49.1 1.5 %collective-permute-start.11 = (f32[1,32,8,128]{3,2,1,0:T(8,128)S(1)}, f32[1,32,8,128]{3,2,1,0:T(8,128)S(1)}, u32[]{:S(2)}, u32[]{:S(2)}) collective-permute-start(f32[1,32,8,128]{3,2,1,0:T(8,128)S(1)} %get-tuple-element.52), channel_id=1, source_target_pairs={{1,0},{0,1},{3,2},{2,3},{5,4},{4,5},{7,6},{6,7},{9,8},{8,9},{11,10... | collective-permute-start | bytes 393224 | tf_op jit(solution)/shard_map/ppermute | solution.py:316
  50.5 1.4 %collective-permute-start.10 = (f32[1,32,8,128]{3,2,1,0:T(8,128)S(1)}, f32[1,32,8,128]{3,2,1,0:T(8,128)S(1)}, u32[]{:S(2)}, u32[]{:S(2)}) collective-permute-start(f32[1,32,8,128]{3,2,1,0:T(8,128)S(1)} %get-tuple-element.51), channel_id=1, source_target_pairs={{1,0},{0,1},{3,2},{2,3},{5,4},{4,5},{7,6},{6,7},{9,8},{8,9},{11,10... | collective-permute-start | bytes 393224 | tf_op jit(solution)/shard_map/ppermute | solution.py:316
